TPU v7x, 32 devices: a whole 2x2x4 slice. The times are simulated.
32 devices in a mesh: ey: 4 (over z), ex: 8 (over y, x, core).
Axes of the slice: x: 2, y: 2, z: 4, core: 2. Of those that a mesh axis runs over, the one named last changes fastest.
Arguments:
- x: bfloat16 [512, 2048], P(('ey', 'ex'))
- kv_k: bfloat16 [512, 256, 4, 128], P(('ey', 'ex'))
- kv_v: bfloat16 [512, 256, 4, 128], P(('ey', 'ex'))
- lens: int32 [512], P(('ey', 'ex'))
- topk_idx: int32 [512, 4], P(('ey', 'ex'))
- gates: float32 [512, 4], P(('ey', 'ex'))
- ln1: bfloat16 [2048], replicated
- wq: bfloat16 [2048, 4096], replicated
- wo: bfloat16 [4096, 2048], replicated
- ln2: bfloat16 [2048], replicated
- ws1: bfloat16 [2048, 5632], replicated
- ws3: bfloat16 [2048, 5632], replicated
- ws2: bfloat16 [5632, 2048], replicated
- w1: bfloat16 [64, 2048, 1408], P(('ey', 'ex'))
- w3: bfloat16 [64, 2048, 1408], P(('ey', 'ex'))
- w2: bfloat16 [64, 1408, 2048], P(('ey', 'ex'))
Outputs:
- output: bfloat16 [512, 2048], P(('ey', 'ex'))
All inputs are finite; a program needn't handle non-finite values.
Results may differ from a plain program's by a relative error of at most 0.0124602.
Values are sent between devices in bfloat16 or wider.
A program may use at most 1 GiB of HBM per device.

v0:
```python
import jax
import jax.numpy as jnp
from jax import lax
from jax.sharding import PartitionSpec as P

EPS = 1e-6
GRP = ("ey", "ex")


def _rms(v, w):
    v32 = v.astype(jnp.float32)
    r = lax.rsqrt(jnp.mean(v32 * v32, axis=-1, keepdims=True) + EPS)
    return (v32 * r * w.astype(jnp.float32)).astype(jnp.bfloat16)


def _swiglu(a, w1, w3, w2):
    z1 = jnp.dot(a, w1, preferred_element_type=jnp.float32)
    z3 = jnp.dot(a, w3, preferred_element_type=jnp.float32)
    g = (jax.nn.silu(z1) * z3).astype(jnp.bfloat16)
    return jnp.dot(g, w2, preferred_element_type=jnp.float32)


def _experts(buf, w1, w3, w2):
    z1 = jnp.einsum("eqd,edf->eqf", buf, w1, preferred_element_type=jnp.float32)
    z3 = jnp.einsum("eqd,edf->eqf", buf, w3, preferred_element_type=jnp.float32)
    g = (jax.nn.silu(z1) * z3).astype(jnp.bfloat16)
    return jnp.einsum("eqf,efd->eqd", g, w2, preferred_element_type=jnp.float32).astype(jnp.bfloat16)


def _attention_block(x, kv_k, kv_v, lens, ln1, wq, wo):
    b, d = x.shape
    _, l, kvh, hd = kv_k.shape
    nh = wq.shape[1] // hd
    a = _rms(x, ln1)
    q = jnp.dot(a, wq, preferred_element_type=jnp.float32).astype(jnp.bfloat16).reshape(b, kvh, nh // kvh, hd)
    s = jnp.einsum("bkgh,blkh->bkgl", q, kv_k, preferred_element_type=jnp.float32) * hd ** -0.5
    s = jnp.where(jnp.arange(l) < lens[:, None, None, None], s, -jnp.inf)
    p = jax.nn.softmax(s, axis=-1).astype(jnp.bfloat16)
    o = jnp.einsum("bkgl,blkh->bkgh", p, kv_v, preferred_element_type=jnp.float32).astype(jnp.bfloat16)
    attn = jnp.dot(o.reshape(b, nh * hd), wo, preferred_element_type=jnp.float32)
    return (x.astype(jnp.float32) + attn).astype(jnp.bfloat16)


def solution(mesh):
    nx = mesh.shape["ex"]
    ndev = mesh.shape["ey"] * nx

    def body(x, kv_k, kv_v, lens, idx, gates, ln1, wq, wo, ln2, ws1, ws3, ws2, w1, w3, w2):
        bdev, d = x.shape
        top = idx.shape[1]
        edev = w1.shape[0]
        cap = bdev - bdev // 8
        rlen = min(bdev * top, edev * cap)
        qrows = ndev * cap
        my = lax.axis_index("ey") * nx + lax.axis_index("ex")
        h = _attention_block(x, kv_k, kv_v, lens, ln1, wq, wo)
        u = _rms(h, ln2)
        shared = _swiglu(u, ws1, ws3, ws2)
        flat = idx.reshape(-1)
        oh = jax.nn.one_hot(flat, edev * ndev, dtype=jnp.int32)
        rank = jnp.sum((jnp.cumsum(oh, axis=0) - oh) * oh, axis=1)
        keep = rank < cap
        dest = flat // edev
        ohd = jax.nn.one_hot(dest, ndev, dtype=jnp.int32) * keep.astype(jnp.int32)[:, None]
        slot = jnp.sum((jnp.cumsum(ohd, axis=0) - ohd) * ohd, axis=1)
        pos = jnp.where(keep, dest * rlen + slot, ndev * rlen)
        tok = jnp.arange(bdev * top) // top
        send_tok = jnp.full((ndev * rlen,), bdev, jnp.int32).at[pos].set(tok, mode="drop")
        send_rows = jnp.take(u, send_tok, axis=0, mode="fill", fill_value=0).reshape(ndev, rlen, d)
        meta = ((flat % edev) * ndev + my) * cap + rank
        send_meta = jnp.full((ndev * rlen,), edev * qrows, jnp.int32).at[pos].set(meta, mode="drop").reshape(ndev, rlen)
        recv_rows = lax.all_to_all(send_rows, GRP, 0, 0, tiled=True)
        recv_meta = lax.all_to_all(send_meta, GRP, 0, 0, tiled=True).reshape(-1)
        buf = jnp.zeros((edev * qrows, d), jnp.bfloat16).at[recv_meta].set(recv_rows.reshape(-1, d), mode="drop")
        out = _experts(buf.reshape(edev, qrows, d), w1, w3, w2).reshape(edev * qrows, d)
        back = jnp.take(out, recv_meta, axis=0, mode="fill", fill_value=0).reshape(ndev, rlen, d)
        ret = lax.all_to_all(back, GRP, 0, 0, tiled=True).reshape(ndev * rlen, d)
        e_rows = jnp.take(ret, pos, axis=0, mode="fill", fill_value=0).reshape(bdev, top, d)
        routed = jnp.sum(gates[:, :, None] * e_rows.astype(jnp.float32), axis=1)
        return (h.astype(jnp.float32) + shared + routed).astype(jnp.bfloat16)

    rows = P(GRP)
    rep = P()
    return jax.shard_map(
        body, mesh=mesh,
        in_specs=(rows, rows, rows, rows, rows, rows, rep, rep, rep, rep, rep, rep, rep, rows, rows, rows),
        out_specs=rows, check_vma=False)
```

profile of v0, /device:TPU:0, one launch (start us, length us, event | category | flops | bytes accessed | tf_op | source)
XLA Modules:
  0.0 343.0 jit_solution(9487175184082111598)
XLA Ops:
  3.2 7.4 %all-to-all-start = ((s32[32,1,28]{2,1,0:T(1,128)}), s32[32,1,28]{2,1,0:T(1,128)S(1)}, u32[]{:S(2)}, u32[]{:S(2)}) async-start(s32[32,1,28]{2,1,0:T(1,128)} %bitcast.3), calls=%async_computation | async-start | bytes 32768 | tf_op jit(solution)/shard_map/all_to_all | solution.py:73
  13.1 8.1 %fusion.23 = bf16[2,8,32,128]{3,1,2,0:T(8,128)(2,1)S(1)} fusion(bf16[2048,4096]{1,0:T(8,128)(2,1)} %param.23, bf16[16,2048]{1,0:T(8,128)(2,1)} %param.16, f32[2048]{0:T(1024)S(1)} %convert_element_type.61, f32[16]{0:T(128)S(1)} %add_rsqrt_fusion.1), kind=kOutput, calls=%fused_computation.31 | convolution fusion | flops 268632064 | bytes 16982080 | tf_op jit(solution)/shard_map/dot_general | solution.py:35
  21.4 3.6 %fusion.59 = (f32[16,4,8]{2,1,0:T(4,128)S(1)}, f32[16,4,8,256]{3,2,1,0:T(8,128)S(1)}) fusion(bf16[16,4,8,128]{3,2,1,0:T(8,128)(2,1)S(1)} %bitcast.48, bf16[16,256,4,128]{3,2,1,0:T(4,128)(2,1)} %param.17, pred[16,256]{1,0:T(8,128)(4,1)S(1)} %iota_compare_fusion.2), kind=kOutput, calls=%fused_computation.111 | convolution fusion | flops 34078976 | bytes 4855808 | tf_op jit(solution)/shard_map/sub | solution.py:38
  24.9 2.9 fusion.20
  27.9 8.2 %multiply_reduce_fusion.1 = (f32[16]{0:T(128)S(1)}, f32[16,2048]{1,0:T(8,128)S(1)}) fusion(bf16[4096,2048]{1,0:T(8,128)(2,1)} %param.24, bf16[2,8,32,128]{3,2,1,0:T(8,128)(2,1)S(1)} %bitcast.46, bf16[16,2048]{1,0:T(8,128)(2,1)S(1)} %copy-done.1), kind=kOutput, calls=%fused_computation.49 | convolution fusion | flops 268632064 | bytes 17104960 | tf_op jit(solution)/shard_map/dot_general | solution.py:40
  36.2 5.0 %gather_fusion = bf16[896,2048]{1,0:T(8,128)(2,1)} fusion(bf16[16,2048]{1,0:T(8,128)(2,1)S(1)} %multiply_convert_fusion.1, s32[1024]{0:T(1024)S(1)} %pad_clamp_fusion.2), kind=kCustom, calls=%fused_computation | custom fusion | bytes 7343616 | tf_op jit(solution)/shard_map/jit(_take)/gather | solution.py:69
  41.2 5.8 %gather.19 = bf16[32,28,2048]{2,1,0:T(8,128)(2,1)} reshape(bf16[896,2048]{1,0:T(8,128)(2,1)} %gather_fusion) | data formatting | bytes 7340032 | tf_op jit(solution)/shard_map/jit(_take)/gather | solution.py:69
  47.2 4.5 %broadcast_select_fusion = bf16[32,28,2048]{2,1,0:T(8,128)(2,1)} fusion(bf16[32,28,2048]{2,1,0:T(8,128)(2,1)} %gather.19, pred[32,28]{1,0:T(8,128)(4,1)S(1)} %broadcast_in_dim.81), kind=kLoop, calls=%fused_computation.15 | loop fusion | flops 1835008 | bytes 7340928 | tf_op jit(solution)/shard_map/jit(_take)/select_n | solution.py:69
  51.7 6.1 %all-to-all-start.1 = ((bf16[32,28,2048]{2,1,0:T(8,128)(2,1)}), bf16[32,28,2048]{2,1,0:T(8,128)(2,1)}, u32[]{:S(2)}, u32[]{:S(2)}) async-start(bf16[32,28,2048]{2,1,0:T(8,128)(2,1)} %broadcast_select_fusion), calls=%async_computation.1 | async-start | bytes 8388608 | tf_op jit(solution)/shard_map/all_to_all | solution.py:72
  59.2 93.4 %all-to-all-done.1 = bf16[32,28,2048]{2,1,0:T(8,128)(2,1)} async-done(((bf16[32,28,2048]{2,1,0:T(8,128)(2,1)}), bf16[32,28,2048]{2,1,0:T(8,128)(2,1)}, u32[]{:S(2)}, u32[]{:S(2)}) %all-to-all-start.1) | async-done | bytes 3670048 | tf_op jit(solution)/shard_map/all_to_all | solution.py:72
  152.6 5.8 %reshape.313 = bf16[896,2048]{1,0:T(8,128)(2,1)} reshape(bf16[32,28,2048]{2,1,0:T(8,128)(2,1)} %all-to-all-done.1) | data formatting | bytes 7340032 | tf_op jit(solution)/shard_map/reshape | solution.py:74
  158.4 10.1 %scatter_custom_fusion.2 = bf16[896,2048]{1,0:T(8,128)(2,1)} fusion(s32[896]{0:T(1024)S(1)} %fusion.47, bf16[896,2048]{1,0:T(8,128)(2,1)} %reshape.313, bf16[]{:T(256)} %constant.125.clone.1), kind=kCustom, calls=%fused_computation.24 | custom fusion | bytes 3670528 | tf_op jit(solution)/shard_map/scatter | solution.py:74
  168.5 9.8 %fusion.63 = f32[2,448,1408]{2,1,0:T(8,128)S(1)} fusion(bf16[2,448,2048]{2,1,0:T(8,128)(2,1)} %bitcast.44, bf16[2,2048,1408]{2,1,0:T(8,128)(2,1)} %param.29), kind=kOutput, calls=%fused_computation.113 | convolution fusion | flops 5167382528 | bytes 20250624 | tf_op jit(solution)/shard_map/eqd,edf->eqf/dot_general | solution.py:24
  178.4 8.9 %multiply_convert_fusion = bf16[2,448,1408]{2,1,0:T(8,128)(2,1)S(1)} fusion(f32[2,448,1408]{2,1,0:T(8,128)S(1)} %fusion.63, bf16[2,448,2048]{2,1,0:T(8,128)(2,1)S(1)} %bitcast.45, bf16[2,2048,1408]{2,1,0:T(8,128)(2,1)} %param.30), kind=kOutput, calls=%fused_computation.9 | convolution fusion | flops 5174951936 | bytes 22773760 | tf_op jit(solution)/shard_map/eqd,edf->eqf/dot_general | solution.py:25
  187.3 7.3 %convolution_convert_fusion.1 = bf16[2,448,2048]{2,1,0:T(8,128)(2,1)} fusion(bf16[2,448,1408]{2,1,0:T(8,128)(2,1)S(1)} %multiply_convert_fusion, bf16[2,1408,2048]{2,1,0:T(8,128)(2,1)S(1)} %bitcast.50), kind=kOutput, calls=%fused_computation.17 | convolution fusion | flops 5169217536 | bytes 17727488 | tf_op jit(solution)/shard_map/eqf,efd->eqd/dot_general | solution.py:27
  194.7 11.3 %gather_fusion.1 = bf16[896,2048]{1,0:T(8,128)(2,1)} fusion(bf16[896,2048]{1,0:T(8,128)(2,1)} %bitcast.43, s32[1024]{0:T(1024)S(1)} %pad_clamp_fusion.1), kind=kCustom, calls=%fused_computation.1 | custom fusion | bytes 7343616 | tf_op jit(solution)/shard_map/jit(_take)/gather | solution.py:76
  206.0 5.8 %gather.21 = bf16[32,28,2048]{2,1,0:T(8,128)(2,1)} reshape(bf16[896,2048]{1,0:T(8,128)(2,1)} %gather_fusion.1) | data formatting | bytes 7340032 | tf_op jit(solution)/shard_map/jit(_take)/gather | solution.py:76
  211.8 4.5 %broadcast_select_fusion.1 = bf16[32,28,2048]{2,1,0:T(8,128)(2,1)} fusion(bf16[32,28,2048]{2,1,0:T(8,128)(2,1)} %gather.21, pred[32,28]{1,0:T(8,128)(4,1)S(1)} %compare_and_fusion), kind=kLoop, calls=%fused_computation.16 | loop fusion | flops 1835008 | bytes 7340928 | tf_op jit(solution)/shard_map/jit(_take)/select_n | solution.py:76
  216.3 3.9 %all-to-all-start.2 = ((bf16[32,28,2048]{2,1,0:T(8,128)(2,1)}), bf16[32,28,2048]{2,1,0:T(8,128)(2,1)}, u32[]{:S(2)}, u32[]{:S(2)}) async-start(bf16[32,28,2048]{2,1,0:T(8,128)(2,1)} %broadcast_select_fusion.1), calls=%async_computation.2 | async-start | bytes 8388608 | tf_op jit(solution)/shard_map/all_to_all | solution.py:77
  220.6 9.2 %fusion.62 = f32[16,5632]{1,0:T(8,128)S(1)} fusion(bf16[16,2048]{1,0:T(8,128)(2,1)S(1)} %multiply_convert_fusion.1, bf16[2048,5632]{1,0:T(8,128)(2,1)} %param.26), kind=kOutput, calls=%fused_computation.112 | convolution fusion | flops 369098752 | bytes 23494656 | tf_op jit(solution)/shard_map/dot_general | solution.py:17
  229.7 85.4 %all-to-all-done.2 = bf16[32,28,2048]{2,1,0:T(8,128)(2,1)} async-done(((bf16[32,28,2048]{2,1,0:T(8,128)(2,1)}), bf16[32,28,2048]{2,1,0:T(8,128)(2,1)}, u32[]{:S(2)}, u32[]{:S(2)}) %all-to-all-start.2) | async-done | bytes 3670048 | tf_op jit(solution)/shard_map/all_to_all | solution.py:77
  315.1 5.8 %reshape.268 = bf16[896,2048]{1,0:T(8,128)(2,1)} reshape(bf16[32,28,2048]{2,1,0:T(8,128)(2,1)} %all-to-all-done.2) | data formatting | bytes 7340032 | tf_op jit(solution)/shard_map/reshape | solution.py:77
  321.0 3.5 %gather_fusion.2 = bf16[64,2048]{1,0:T(8,128)(2,1)S(1)} fusion(bf16[896,2048]{1,0:T(8,128)(2,1)} %reshape.268, s32[1024]{0:T(1024)S(1)} %pad_clamp_fusion), kind=kCustom, calls=%fused_computation.2 | custom fusion | bytes 524544 | tf_op jit(solution)/shard_map/jit(_take)/gather | solution.py:78
  325.1 17.9 %fusion.7 = bf16[16,2048]{1,0:T(8,128)(2,1)} fusion(f32[16,2048]{1,0:T(8,128)S(1)} %multiply_reduce_fusion, f32[16,2048]{1,0:T(8,128)S(1)} %get-tuple-element.12, bf16[5632,2048]{1,0:T(8,128)(2,1)} %param.28, bf16[16,2048]{1,0:T(8,128)(2,1)S(1)} %multiply_convert_fusion.1, bf16[2048,5632]{1,0:T(8,128)(2,1)} %param.27, f32[16,5632]{1,0:T(8,128)S(1)} %fusion.62), kind=kOutput, calls=%fused_computation.21 | convolution fusion | flops 738836480 | bytes 46891008 | tf_op jit(solution)/shard_map/dot_general | solution.py:20
  (59 shorter events, 8.3 us)
Async XLA Ops:
  3.2 48.5 %all-to-all-start = ((s32[32,1,28]{2,1,0:T(1,128)}), s32[32,1,28]{2,1,0:T(1,128)S(1)}, u32[]{:S(2)}, u32[]{:S(2)}) async-start(s32[32,1,28]{2,1,0:T(1,128)} %bitcast.3), calls=%async_computation | async-start | bytes 32768 | tf_op jit(solution)/shard_map/all_to_all | solution.py:73
  13.1 8.2 %copy-start.4 = (s32[16]{0:T(128)S(1)}, s32[16]{0:T(128)}, u32[]{:S(2)}) copy-start(s32[16]{0:T(128)} %param.19) | copy-start | bytes 196
  24.9 3.0 copy-start.1
  27.9 8.2 %copy-start.2 = (bf16[2048]{0:T(1024)(128)(2,1)S(1)}, bf16[2048]{0:T(1024)(128)(2,1)}, u32[]{:S(2)}) copy-start(bf16[2048]{0:T(1024)(128)(2,1)} %param.25) | copy-start | bytes 12292
  51.7 100.9 %all-to-all-start.1 = ((bf16[32,28,2048]{2,1,0:T(8,128)(2,1)}), bf16[32,28,2048]{2,1,0:T(8,128)(2,1)}, u32[]{:S(2)}, u32[]{:S(2)}) async-start(bf16[32,28,2048]{2,1,0:T(8,128)(2,1)} %broadcast_select_fusion), calls=%async_computation.1 | async-start | bytes 8388608 | tf_op jit(solution)/shard_map/all_to_all | solution.py:72
  168.5 9.8 %copy-start = (bf16[896,2048]{1,0:T(8,128)(2,1)S(1)}, bf16[896,2048]{1,0:T(8,128)(2,1)}, u32[]{:S(2)}) copy-start(bf16[896,2048]{1,0:T(8,128)(2,1)} %scatter_custom_fusion.2) | copy-start | bytes 11010052
  168.5 18.8 %slice-start = ((s8[11534336]{0:T(1024)(128)(4,1)}), s8[4194304]{0:T(1024)(128)(4,1)S(1)}, s32[]{:S(2)}) async-start(s8[11534336]{0:T(1024)(128)(4,1)} %bitcast.49), calls=%async_computation.3 | async-start | bytes 8388608
  178.4 8.9 %slice-start.1 = ((s8[11534336]{0:T(1024)(128)(4,1)}), s8[4194304]{0:T(1024)(128)(4,1)S(1)}, s32[]{:S(2)}) async-start(s8[11534336]{0:T(1024)(128)(4,1)} %bitcast.49), calls=%async_computation.4 | async-start | bytes 8388608
  178.4 8.9 %slice-start.2 = ((s8[11534336]{0:T(1024)(128)(4,1)}), s8[3145728]{0:T(1024)(128)(4,1)S(1)}, s32[]{:S(2)}) async-start(s8[11534336]{0:T(1024)(128)(4,1)} %bitcast.49), calls=%async_computation.5 | async-start | bytes 6291456
  216.3 4.1 %copy-start.3 = (f32[16,4]{0,1:T(4,128)S(1)}, f32[16,4]{0,1:T(4,128)}, u32[]{:S(2)}) copy-start(f32[16,4]{0,1:T(4,128)} %param.21) | copy-start | bytes 772
  216.3 98.8 %all-to-all-start.2 = ((bf16[32,28,2048]{2,1,0:T(8,128)(2,1)}), bf16[32,28,2048]{2,1,0:T(8,128)(2,1)}, u32[]{:S(2)}, u32[]{:S(2)}) async-start(bf16[32,28,2048]{2,1,0:T(8,128)(2,1)} %broadcast_select_fusion.1), calls=%async_computation.2 | async-start | bytes 8388608 | tf_op jit(solution)/shard_map/all_to_all | solution.py:77
where the time goes:
time: 344 us; the launch traced here: 343 us
  waiting for transfers between devices  179 us (52%)
  matrix products  75.9 us (22%)
  local copies, waits for them, and re-layouts  57.6 us (17%)
  starting transfers between devices  17.4 us (5%)
  other arithmetic  12.9 us (4%)
    all_to_all x1, waiting for transfers between devices, body(): recv_rows = lax.all_to_all(send_rows, GRP, 0, 0, tiled=True)  93.4 us
    all_to_all x1, waiting for transfers between devices, body(): ret = lax.all_to_all(back, GRP, 0, 0, tiled=True).reshape(ndev * rlen, d)  85.4 us
    dot_general x1, matrix products, _swiglu(): return jnp.dot(g, w2, preferred_element_type=jnp.float32)  17.9 us
    gather x2, local copies, waits for them, and re-layouts, body(): jnp.take(out, recv_meta, axis=0, mode='fill', fill_value=0)  17.1 us
    gather x2, local copies, waits for them, and re-layouts, body(): jnp.take(u, send_tok, axis=0, mode='fill', fill_value=0)  10.8 us
    scatter x1, local copies, waits for them, and re-layouts, body(): jnp.zeros((edev * qrows, d), jnp.bfloat16).at[recv_meta]  10.1 us
    dot_general x1, matrix products, _experts(): z1 = jnp.einsum('eqd,edf->eqf', buf, w1, preferred_element_type=jnp.float32)  9.81 us
    dot_general x1, matrix products, _swiglu(): z1 = jnp.dot(a, w1, preferred_element_type=jnp.float32)  9.17 us
  transfers between devices with their start and end apart: 3, of which 2 were waited for; matrix products, arithmetic and copies ran while one was open for 15% of the time, Pallas kernels for 0%

commit v1 on v0

v1 whole, which is shorter than its diff:
```python
import functools

import jax
import jax.numpy as jnp
from jax import lax
from jax.experimental import pallas as pl
from jax.experimental.pallas import tpu as pltpu
from jax.sharding import PartitionSpec as P

EPS = 1e-6
GRP = ("ey", "ex")
MESH = pl.DeviceIdType.MESH
BF16, F32 = jnp.bfloat16, jnp.float32

CHUNKS = ((0, 2), (2, 1), (3, 1))
SHARED_DEVS = 22


def _rms(v, w):
    v32 = v.astype(F32)
    r = lax.rsqrt(jnp.mean(v32 * v32, axis=-1, keepdims=True) + EPS)
    return (v32 * r * w.astype(F32)).astype(BF16)


def _attention_block(x, kv_k, kv_v, lens, ln1, wq, wo):
    b, d = x.shape
    _, l, kvh, hd = kv_k.shape
    nh = wq.shape[1] // hd
    a = _rms(x, ln1)
    q = jnp.dot(a, wq, preferred_element_type=F32).astype(BF16).reshape(b, kvh, nh // kvh, hd)
    s = jnp.einsum("bkgh,blkh->bkgl", q, kv_k, preferred_element_type=F32) * hd ** -0.5
    s = jnp.where(jnp.arange(l) < lens[:, None, None, None], s, -jnp.inf)
    p = jax.nn.softmax(s, axis=-1).astype(BF16)
    o = jnp.einsum("bkgl,blkh->bkgh", p, kv_v, preferred_element_type=F32).astype(BF16)
    attn = jnp.dot(o.reshape(b, nh * hd), wo, preferred_element_type=F32)
    return (x.astype(F32) + attn).astype(BF16)


def _moe_kernel(h_ref, ln_ref, idx_ref, gate_ref, s1_hbm, s3_hbm, s2_hbm, w1_hbm, w3_hbm, w2_hbm, y_ref,
                U, GW, GB, Pb, R1, R2x, R2y, R3x, R3y, R4, G, GS, W1, W3, W2, S1, S3, S2,
                wsem, ag_s, ag_r, gw_s, gw_r, rs_s, rs_r):
    z = lax.axis_index("ey")
    ex = lax.axis_index("ex")
    c = lax.rem(ex, 2)
    xx = lax.rem(lax.div(ex, 2), 2)
    yy = lax.div(ex, 4)
    dev = z * 8 + ex
    bdev, d = h_ref.shape
    f = W1.shape[2]
    cap = bdev - bdev // 8
    half = d // 2
    H0, H1 = pl.ds(0, half), pl.ds(half, half)
    ALL = pl.ds(0, d)
    core = (z, ex + 1 - 2 * c)
    xn = (z, ex + 2 - 4 * xx)
    yn = (z, ex + 4 - 8 * yy)
    zp = {1: (z + 1 - 2 * lax.rem(z, 2), ex), 2: (z + 2 - 4 * lax.div(z, 2), ex), 3: (3 - z, ex)}

    def rows(k, dc, dq, n=1):
        return pl.ds(((k * 2 + dc) * 4 + dq) * bdev, n * bdev)

    loads = {}

    def load(name, i, src, dst):
        cp = pltpu.make_async_copy(src, dst, wsem.at[i])
        cp.start()
        loads[name] = cp

    load("w1_0", 0, w1_hbm.at[0], W1.at[0])
    load("w3_0", 1, w3_hbm.at[0], W3.at[0])
    load("w1_1", 2, w1_hbm.at[1], W1.at[1])
    load("w3_1", 3, w3_hbm.at[1], W3.at[1])
    scol = pl.ds(pl.multiple_of(lax.rem(dev, SHARED_DEVS) * 256, 256), 256)
    load("s1", 6, s1_hbm.at[:, scol], S1)
    load("s3", 7, s3_hbm.at[:, scol], S3)
    load("s2", 8, s2_hbm.at[scol, :], S2)
    load("w2_0", 4, w2_hbm.at[0], W2.at[0])
    load("w2_1", 5, w2_hbm.at[1], W2.at[1])
    waited = set()

    def need(*names):
        for n in names:
            if n not in waited:
                waited.add(n)
                loads[n].wait()

    u = _rms(h_ref[...], ln_ref[...])
    U[rows(0, 0, 0), :] = u
    lane = lax.broadcasted_iota(jnp.int32, (bdev, 128), 1)
    oh = jnp.zeros((bdev, 128), F32)
    gm = jnp.zeros((bdev, 128), F32)
    for j in range(idx_ref.shape[1]):
        hit = idx_ref[:, j:j + 1] == lane
        oh = oh + jnp.where(hit, 1.0, 0.0)
        gm = gm + jnp.where(hit, gate_ref[:, j:j + 1], 0.0)
    r_i = lax.broadcasted_iota(jnp.int32, (bdev, bdev), 0)
    c_i = lax.broadcasted_iota(jnp.int32, (bdev, bdev), 1)
    tril = jnp.where(c_i < r_i, 1.0, 0.0)
    rank = jnp.dot(tril.astype(BF16), oh.astype(BF16), preferred_element_type=F32)
    GW[rows(0, 0, 0), :] = jnp.where(rank < cap - 0.5, gm, 0.0)

    barrier = pltpu.get_barrier_semaphore()
    for n in (core, xn, yn, zp[1], zp[2], zp[3]):
        pl.semaphore_signal(barrier, inc=1, device_id=n, device_id_type=MESH)
    pl.semaphore_wait(barrier, 6)

    def send(src, dst, ss, rs, to):
        cp = pltpu.make_async_remote_copy(src_ref=src, dst_ref=dst, send_sem=ss, recv_sem=rs,
                                          device_id=to, device_id_type=MESH)
        cp.start()
        return cp

    sent = []

    ag = {}

    def ag_send(key, i, src_rows, dst_rows, cols, to):
        cp = send(U.at[src_rows, cols], U.at[dst_rows, cols], ag_s.at[i], ag_r.at[i], to)
        ag[key] = cp
        sent.append(cp)

    gw = {}

    def gw_send(key, i, src_rows, dst_rows, to):
        cp = send(GW.at[src_rows, :], GW.at[dst_rows, :], gw_s.at[i], gw_r.at[i], to)
        gw[key] = cp
        sent.append(cp)

    def a2(k):
        ag_send(("2x", k), 3 + k * 6, rows(k, 0, 0), rows(k, 0, 1), H0, xn)
        ag_send(("2y", k), 4 + k * 6, rows(k, 0, 0), rows(k, 0, 2), H1, yn)
        gw_send(("2", k), 3 + k * 3, rows(k, 0, 0), rows(k, 0, 1), xn)

    def a3(k):
        ag[("2x", k)].wait_recv()
        ag_send(("3y", k), 5 + k * 6, rows(k, 0, 0, 2), rows(k, 0, 2, 2), H0, yn)
        ag[("2y", k)].wait_recv()
        ag_send(("3x", k), 6 + k * 6, rows(k, 0, 0), rows(k, 0, 1), H1, xn)
        ag_send(("3d", k), 7 + k * 6, rows(k, 0, 2), rows(k, 0, 3), H1, xn)
        gw[("2", k)].wait_recv()
        gw_send(("3", k), 4 + k * 3, rows(k, 0, 0, 2), rows(k, 0, 2, 2), yn)

    def a4(k):
        for n in ("3y", "3x", "3d"):
            ag[(n, k)].wait_recv()
        ag_send(("4", k), 8 + k * 6, rows(k, 0, 0, 4), rows(k, 1, 0, 4), ALL, core)
        gw[("3", k)].wait_recv()
        gw_send(("4", k), 5 + k * 3, rows(k, 0, 0, 4), rows(k, 1, 0, 4), core)

    def a5(k):
        ag[("4", k)].wait_recv()
        gw[("4", k)].wait_recv()

    def zwait(k):
        ag[("z", k)].wait_recv()
        gw[("z", k)].wait_recv()
        a2(k)

    for k in (1, 2, 3):
        ag_send(("z", k), k - 1, rows(0, 0, 0), rows(k, 0, 0), ALL, zp[k])
        gw_send(("z", k), k - 1, rows(0, 0, 0), rows(k, 0, 0), zp[k])
    a2(0)
    zwait(1)
    a3(0)
    zwait(2)
    a3(1)
    a4(0)
    zwait(3)
    a3(2)
    a4(1)
    a5(0)

    rs = {}

    def rs_send(key, i, src, dst, to):
        cp = send(src, dst, rs_s.at[i], rs_r.at[i], to)
        rs[key] = cp
        sent.append(cp)

    def s1(k):
        rs_send(("1", k), k * 8, Pb.at[rows(k, 1, 0, 4), :], R1.at[pl.ds(k * 64, 64), :], core)

    def s2(k):
        rs[("1", k)].wait_recv()
        Pb[rows(k, 0, 0, 4), :] = Pb[rows(k, 0, 0, 4), :] + R1[pl.ds(k * 64, 64), :]
        rs_send(("2y", k), k * 8 + 1, Pb.at[rows(k, 0, 2, 2), H0], R2y.at[pl.ds(k * 32, 32), :], yn)
        rs_send(("2x", k), k * 8 + 2, Pb.at[rows(k, 0, 1), H1], R2x.at[pl.ds(k * 32, 16), :], xn)
        rs_send(("2d", k), k * 8 + 3, Pb.at[rows(k, 0, 3), H1], R2x.at[pl.ds(k * 32 + 16, 16), :], xn)

    def s3(k):
        rs[("2y", k)].wait_recv()
        Pb[rows(k, 0, 0, 2), H0] = Pb[rows(k, 0, 0, 2), H0] + R2y[pl.ds(k * 32, 32), :]
        rs_send(("3x", k), k * 8 + 4, Pb.at[rows(k, 0, 1), H0], R3x.at[pl.ds(k * 16, 16), :], xn)
        rs[("2x", k)].wait_recv()
        rs[("2d", k)].wait_recv()
        Pb[rows(k, 0, 2), H1] = Pb[rows(k, 0, 2), H1] + R2x[pl.ds(k * 32 + 16, 16), :]
        rs_send(("3y", k), k * 8 + 5, Pb.at[rows(k, 0, 2), H1], R3y.at[pl.ds(k * 16, 16), :], yn)
        Pb[rows(k, 0, 0), H1] = Pb[rows(k, 0, 0), H1] + R2x[pl.ds(k * 32, 16), :]

    def s4(k):
        rs[("3x", k)].wait_recv()
        Pb[rows(k, 0, 0), H0] = Pb[rows(k, 0, 0), H0] + R3x[pl.ds(k * 16, 16), :]
        rs[("3y", k)].wait_recv()
        Pb[rows(k, 0, 0), H1] = Pb[rows(k, 0, 0), H1] + R3y[pl.ds(k * 16, 16), :]
        if k:
            rs_send(("4", k), k * 8 + 6, Pb.at[rows(k, 0, 0), :], R4.at[pl.ds(k * 16, 16), :], zp[k])

    def up(uval, wa, wb, gdst, tiles):
        def step(t, _):
            col = pl.ds(pl.multiple_of(t * 128, 128), 128)
            w = jnp.concatenate([wa[:, col], wb[:, col]], axis=1)
            zz = jnp.dot(uval[...], w, preferred_element_type=F32)
            z1, z3 = zz[:, :128], zz[:, 128:]
            gdst[:, col] = (z1 * jax.nn.sigmoid(z1) * z3).astype(BF16)
            return 0
        lax.fori_loop(0, tiles, step, 0)

    def chunk(k0, n, hooks):
        m = n * 8 * bdev
        cr = pl.ds(k0 * 8 * bdev, m)
        mr = pl.ds(0, m)
        uv = U.at[cr, :]
        lanes = lax.broadcasted_iota(jnp.int32, (m, 128), 1)
        for e in range(2):
            gv = jnp.sum(jnp.where(lanes == dev * 2 + e, GW[cr, :], 0.0), axis=1, keepdims=True)
            GB[e, mr, :] = jnp.broadcast_to(gv, (m, 128))
        for e in range(2):
            need(f"w1_{e}", f"w3_{e}")
            up(uv, W1.at[e], W3.at[e], G.at[e, mr, :], f // 128)
            hooks[e]()
        need("s1", "s3")

        @pl.when(dev < SHARED_DEVS)
        def _():
            up(uv, S1, S3, GS.at[mr, :], 2)

        @pl.when(dev >= SHARED_DEVS)
        def _():
            GS[mr, :] = jnp.zeros((m, 256), BF16)

        need("w2_0", "w2_1", "s2")

        def step(t, _):
            col = pl.ds(pl.multiple_of(t * 256, 256), 256)
            acc = jnp.dot(GS[mr, :], S2[:, col], preferred_element_type=F32)
            for e in range(2):
                r = jnp.dot(G[e, mr, :], W2[e, :, col], preferred_element_type=F32).astype(BF16).astype(F32)
                g = GB[e, mr, :]
                g = jnp.concatenate([g, g], axis=1)
                acc = acc + jnp.where(g > 0, g * r, 0.0)
            Pb[cr, col] = acc
            return 0
        lax.fori_loop(0, 4, step, 0)
        hooks[2]()
        lax.fori_loop(4, 8, step, 0)
        hooks[3]()

    def nop():
        pass

    a5(1)

    def h_a():
        a3(3)
        a4(2)

    def h_b():
        a5(2)
        a4(3)

    chunk(0, 2, (h_a, h_b, lambda: a5(3), lambda: (s1(0), s1(1))))
    chunk(2, 1, (lambda: (s2(0), s2(1)), lambda: (s3(0), s3(1)), lambda: (s4(0), s4(1)), lambda: s1(2)))
    chunk(3, 1, (lambda: s2(2), lambda: s3(2), lambda: s4(2), lambda: s1(3)))
    s2(3)
    s3(3)
    s4(3)

    acc = h_ref[...].astype(F32) + Pb[rows(0, 0, 0), :]
    for k in (1, 2, 3):
        rs[("4", k)].wait_recv()
        acc = acc + R4[pl.ds(k * 16, 16), :]
    y_ref[...] = acc.astype(BF16)
    for cp in sent:
        cp.wait_send()


def solution(mesh):
    def body(x, kv_k, kv_v, lens, idx, gates, ln1, wq, wo, ln2, ws1, ws3, ws2, w1, w3, w2):
        bdev, d = x.shape
        f = w1.shape[2]
        rows = bdev * 32
        h = _attention_block(x, kv_k, kv_v, lens, ln1, wq, wo)
        vm = pl.BlockSpec(memory_space=pltpu.VMEM)
        hbm = pl.BlockSpec(memory_space=pl.ANY)
        mmax = max(n for _, n in CHUNKS) * 8 * bdev
        return pl.pallas_call(
            _moe_kernel,
            out_shape=jax.ShapeDtypeStruct((bdev, d), BF16),
            in_specs=[vm] * 4 + [hbm] * 6,
            out_specs=vm,
            scratch_shapes=[
                pltpu.VMEM((rows, d), BF16),
                pltpu.VMEM((rows, 128), F32),
                pltpu.VMEM((2, mmax, 128), F32),
                pltpu.VMEM((rows, d), F32),
                pltpu.VMEM((rows // 2, d), F32),
                pltpu.VMEM((128, d // 2), F32),
                pltpu.VMEM((128, d // 2), F32),
                pltpu.VMEM((64, d // 2), F32),
                pltpu.VMEM((64, d // 2), F32),
                pltpu.VMEM((64, d), F32),
                pltpu.VMEM((2, mmax, f), BF16),
                pltpu.VMEM((mmax, 256), BF16),
                pltpu.VMEM((2, d, f), BF16),
                pltpu.VMEM((2, d, f), BF16),
                pltpu.VMEM((2, f, d), BF16),
                pltpu.VMEM((d, 256), BF16),
                pltpu.VMEM((d, 256), BF16),
                pltpu.VMEM((256, d), BF16),
                pltpu.SemaphoreType.DMA((9,)),
                pltpu.SemaphoreType.DMA((28,)),
                pltpu.SemaphoreType.DMA((28,)),
                pltpu.SemaphoreType.DMA((16,)),
                pltpu.SemaphoreType.DMA((16,)),
                pltpu.SemaphoreType.DMA((32,)),
                pltpu.SemaphoreType.DMA((32,)),
            ],
            compiler_params=pltpu.CompilerParams(
                collective_id=0, has_side_effects=True, vmem_limit_bytes=60 * 1024 * 1024
            ),
        )(h, ln2.reshape(1, d), idx, gates, ws1, ws3, ws2, w1, w3, w2)

    rows = P(GRP)
    rep = P()
    return jax.shard_map(
        body, mesh=mesh,
        in_specs=(rows, rows, rows, rows, rows, rows, rep, rep, rep, rep, rep, rep, rep, rows, rows, rows),
        out_specs=rows, check_vma=False)
```

time: 344 us -> 110 us (0.32)
  waiting for transfers between devices: 179 us -> 0 us
  Pallas kernels: 0 us -> 81.2 us
  local copies, waits for them, and re-layouts: 57.6 us -> 3.48 us
  matrix products: 75.9 us -> 23.4 us
  starting transfers between devices: 17.4 us -> 0 us
  other arithmetic: 12.9 us -> 1.74 us
    all_to_all x3 -> x0, waiting for transfers between devices: 179 us -> none  [the longest x1 93.4 us: body(): recv_rows = lax.all_to_all(send_rows, GRP, 0, 0, tiled=True)]
    pallas_call x0 -> x1, Pallas kernels: none -> 81.2 us  [body(): pl.pallas_call(_moe_kernel, out_shape=jax.ShapeDtypeStruct((bdev, d), BF1...]
    dot_general x8 -> x3, matrix products: 72.4 us -> 19.8 us  [the longest x1 8.72 us: _attention_block(): attn = jnp.dot(o.reshape(b, nh * hd), wo, preferred_element_type=F32)]
    gather x6 -> x0, local copies, waits for them, and re-layouts: 31.6 us -> none  [the longest x2 17.1 us: body(): jnp.take(out, recv_meta, axis=0, mode='fill', fill_value=0)]
    all_to_all x3 -> x0, starting transfers between devices: 17.4 us -> none  [the longest x1 7.36 us: body(): recv_meta = lax.all_to_all(send_meta, GRP, 0, 0, tiled=True).reshape(-1)]
    scatter x3 -> x0, local copies, waits for them, and re-layouts: 11.7 us -> none  [the longest x1 10.1 us: body(): jnp.zeros((edev * qrows, d), jnp.bfloat16).at[recv_meta]]
    reshape x4 -> x1, local copies, waits for them, and re-layouts: 11.9 us -> 0.6 us  [body(): ln2.reshape(1, d)]
    select_n x6 -> x0, other arithmetic: 9.08 us -> none  [the longest x2 4.53 us: body(): jnp.take(out, recv_meta, axis=0, mode='fill', fill_value=0)]
  transfers between devices with their start and end apart: 3 -> 0, of which waited for: 2 -> 0; matrix products, arithmetic and copies ran while one was open for 15% -> 0% of each run, Pallas kernels for 0% -> 0%
where the time goes in v1:
time: 110 us
  Pallas kernels  81.2 us (74%)
  matrix products  23.4 us (21%)
  local copies, waits for them, and re-layouts  3.48 us (3%)
  other arithmetic  1.74 us (2%)
    pallas_call x1, Pallas kernels, body(): pl.pallas_call(_moe_kernel, out_shape=jax.ShapeDtypeStruct((bdev, d), BF1...  81.2 us
    dot_general x1, matrix products, _attention_block(): attn = jnp.dot(o.reshape(b, nh * hd), wo, preferred_element_type=F32)  8.72 us
    dot_general x1, matrix products, _attention_block(): jnp.dot(a, wq, preferred_element_type=F32).astype(BF16)  8.17 us
    sub x1, matrix products, _attention_block(): p = jax.nn.softmax(s, axis=-1).astype(BF16)  3.56 us
    dot_general x1, matrix products, _attention_block(): jnp.einsum('bkgl,blkh->bkgh', p, kv_v, preferred_element_type=F32)  2.92 us
    unnamed x14, local copies, waits for them, and re-layouts  2.88 us

profile of v1, /device:TPU:0, one launch (start us, length us, event | category | flops | bytes accessed | tf_op | source)
XLA Modules:
  0.0 109.8 jit_solution(3679093821023497295)
XLA Ops:
  0.0 0.7 convert_element_type.23
  0.7 1.0 fusion.19
  1.7 0.0 copy-start.4
  1.7 0.0 copy-start
  1.7 8.2 %fusion.17 = bf16[2,8,32,128]{3,1,2,0:T(8,128)(2,1)S(1)} fusion(bf16[2048,4096]{1,0:T(8,128)(2,1)} %param.23, bf16[16,2048]{1,0:T(8,128)(2,1)} %param.16, f32[2048]{0:T(1024)S(1)} %convert_element_type.23, f32[16]{0:T(128)S(1)} %add_rsqrt_fusion), kind=kOutput, calls=%fused_computation.13 | convolution fusion | flops 268632064 | bytes 16982080 | tf_op jit(solution)/shard_map/dot_general | solution.py:30
  9.9 0.0 copy-done.4
  9.9 0.1 iota_compare_fusion
  10.0 3.6 %fusion.27 = (f32[16,4,8]{2,1,0:T(4,128)S(1)}, f32[16,4,8,256]{3,2,1,0:T(8,128)S(1)}) fusion(bf16[16,4,8,128]{3,2,1,0:T(8,128)(2,1)S(1)} %bitcast.13, bf16[16,256,4,128]{3,2,1,0:T(4,128)(2,1)} %param.17, pred[16,256]{1,0:T(8,128)(4,1)S(1)} %iota_compare_fusion), kind=kOutput, calls=%fused_computation.27 | convolution fusion | flops 34078976 | bytes 4855808 | tf_op jit(solution)/shard_map/sub | solution.py:33
  13.5 2.9 %fusion.14 = bf16[16,4,8,128]{3,2,1,0:T(8,128)(2,1)S(1)} fusion(bf16[16,256,4,128]{3,2,1,0:T(4,128)(2,1)} %param.18, f32[16,4,8,256]{3,2,1,0:T(8,128)S(1)} %get-tuple-element.6, f32[16,4,8]{2,1,0:T(4,128)S(1)} %get-tuple-element.5), kind=kOutput, calls=%fused_computation.12 | convolution fusion | flops 33882112 | bytes 4851712 | tf_op jit(solution)/shard_map/bkgl,blkh->bkgh/dot_general | solution.py:34
  16.4 0.0 copy-done
  16.4 0.0 copy-start.2
  16.5 0.0 copy-start.3
  16.5 0.0 copy-start.1
  16.5 8.7 %fusion.5.h_ref = bf16[16,2048]{1,0:T(8,128)(2,1)} fusion(bf16[4096,2048]{1,0:T(8,128)(2,1)} %param.24, bf16[16,2048]{1,0:T(8,128)(2,1)S(1)} %copy-done, bf16[2,8,32,128]{3,2,1,0:T(8,128)(2,1)S(1)} %bitcast.12), kind=kOutput, calls=%fused_computation.7 | convolution fusion | flops 268533760 | bytes 17039360 | tf_op jit(solution)/shard_map/dot_general | solution.py:35
  25.2 0.0 copy-done.2
  25.2 0.7 copy.19.idx_ref
  25.9 0.0 copy-done.3
  25.9 0.7 copy.20.gate_ref
  26.6 0.0 copy-done.1
  26.6 0.6 reshape.43.ln_ref
  27.2 81.2 %shard_map.154 = bf16[16,2048]{1,0:T(8,128)(2,1)} custom-call(bf16[16,2048]{1,0:T(8,128)(2,1)} %fusion.5.h_ref, bf16[1,2048]{1,0:T(2,128)(2,1)} %reshape.43.ln_ref, s32[16,4]{1,0:T(8,128)} %copy.19.idx_ref, f32[16,4]{1,0:T(8,128)} %copy.20.gate_ref, bf16[2048,5632]{1,0:T(8,128)(2,1)} %s1_hbm.1, bf16[2048,5632]{1,0:T(8,128)(2,1)} %s3_hbm.1, ...), custom_call_target="tpu_custom_call" | custom-call | tf_op jit(solution)/shard_map/pallas_call | solution.py:296
  108.3 1.5 %copy.40 = bf16[16,2048]{1,0:T(8,128)(2,1)} copy(bf16[16,2048]{1,0:T(8,128)(2,1)} %shard_map.154) | data formatting | bytes 131072
  (2 shorter events, 0.0 us)
Async XLA Ops:
  1.7 8.2 %copy-start.4 = (s32[16]{0:T(128)S(1)}, s32[16]{0:T(128)}, u32[]{:S(2)}) copy-start(s32[16]{0:T(128)} %param.19) | copy-start | bytes 196
  1.7 14.8 %copy-start = (bf16[16,2048]{1,0:T(8,128)(2,1)S(1)}, bf16[16,2048]{1,0:T(8,128)(2,1)}, u32[]{:S(2)}) copy-start(bf16[16,2048]{1,0:T(8,128)(2,1)} %param.16) | copy-start | bytes 196612
  16.4 8.8 %copy-start.2 = (s32[16,4]{0,1:T(4,128)S(1)}, s32[16,4]{0,1:T(4,128)}, u32[]{:S(2)}) copy-start(s32[16,4]{0,1:T(4,128)} %param.20) | copy-start | bytes 772
  16.5 9.4 %copy-start.3 = (f32[16,4]{0,1:T(4,128)S(1)}, f32[16,4]{0,1:T(4,128)}, u32[]{:S(2)}) copy-start(f32[16,4]{0,1:T(4,128)} %param.21) | copy-start | bytes 772
  16.5 10.1 %copy-start.1 = (bf16[2048]{0:T(1024)(128)(2,1)S(1)}, bf16[2048]{0:T(1024)(128)(2,1)}, u32[]{:S(2)}) copy-start(bf16[2048]{0:T(1024)(128)(2,1)} %param.25) | copy-start | bytes 12292

commit v2 on v1

v2 whole, which is shorter than its diff:
```python
import functools

import jax
import jax.numpy as jnp
from jax import lax
from jax.experimental import pallas as pl
from jax.experimental.pallas import tpu as pltpu
from jax.sharding import PartitionSpec as P

EPS = 1e-6
GRP = ("ey", "ex")
MESH = pl.DeviceIdType.MESH
BF16, F32 = jnp.bfloat16, jnp.float32

SHARED_DEVS = 22
CHUNKS = ((1, 1), (2, 1), (3, 1), (0, 1))
UNROLL, UNROLL2 = 8, 4


def HOOKS(ci, a2, zwait, a3, a4, a5, s1, s2, s3, s4):
    order = [k for k, _ in CHUNKS]
    k = order[ci]
    ev = {i: [] for i in range(5)}
    if ci == 0:
        ev[0] += [(a3, 3), (a4, 2)]
        ev[1] += [(a4, 0)]
        ev[2] += [(a4, 3)]
    if ci >= 2:
        ev[1] += [(s4, order[ci - 2], 0), (s4, order[ci - 2], 1)]
    if ci >= 1:
        ev[0] += [(s2, order[ci - 1], 0), (s2, order[ci - 1], 1)]
    ev[3] += [(s1, k, 0)]
    ev[4] += [(s1, k, 1)]
    if ci >= 1:
        ev[4] += [(s3, order[ci - 1], 0), (s3, order[ci - 1], 1)]
    return ev


def _rms(v, w):
    v32 = v.astype(F32)
    r = lax.rsqrt(jnp.mean(v32 * v32, axis=-1, keepdims=True) + EPS)
    return (v32 * r * w.astype(F32)).astype(BF16)


def _attention_block(x, kv_k, kv_v, lens, ln1, wq, wo):
    b, d = x.shape
    _, l, kvh, hd = kv_k.shape
    nh = wq.shape[1] // hd
    a = _rms(x, ln1)
    q = jnp.dot(a, wq, preferred_element_type=F32).astype(BF16).reshape(b, kvh, nh // kvh, hd)
    s = jnp.einsum("bkgh,blkh->bkgl", q, kv_k, preferred_element_type=F32) * hd ** -0.5
    s = jnp.where(jnp.arange(l) < lens[:, None, None, None], s, -jnp.inf)
    p = jax.nn.softmax(s, axis=-1).astype(BF16)
    o = jnp.einsum("bkgl,blkh->bkgh", p, kv_v, preferred_element_type=F32).astype(BF16)
    attn = jnp.dot(o.reshape(b, nh * hd), wo, preferred_element_type=F32)
    return (x.astype(F32) + attn).astype(BF16)


def _moe_kernel(h_ref, ln_ref, idx_ref, gate_ref, s1_hbm, s3_hbm, s2_hbm, w1_hbm, w3_hbm, w2_hbm, y_ref,
                U, GW, GB, Pb, R1, R2x, R2y, R3x, R3y, R4, G, W13, W2, S2,
                wsem, w2sem, s2sem, ag_s, ag_r, gw_s, gw_r, rs_s, rs_r):
    z = lax.axis_index("ey")
    ex = lax.axis_index("ex")
    c = lax.rem(ex, 2)
    xx = lax.rem(lax.div(ex, 2), 2)
    yy = lax.div(ex, 4)
    dev = z * 8 + ex
    bdev, d = h_ref.shape
    f = w1_hbm.shape[2]
    cap = bdev - bdev // 8
    half = d // 2
    H0, H1 = pl.ds(0, half), pl.ds(half, half)
    ALL = pl.ds(0, d)
    core = (z, ex + 1 - 2 * c)
    xn = (z, ex + 2 - 4 * xx)
    yn = (z, ex + 4 - 8 * yy)
    zp = {1: (z + 1 - 2 * lax.rem(z, 2), ex), 2: (z + 2 - 4 * lax.div(z, 2), ex), 3: (3 - z, ex)}

    def rows(k, dc, dq, n=1):
        return pl.ds(((k * 2 + dc) * 4 + dq) * bdev, n * bdev)

    nt = f // 128
    L0, L1 = pl.ds(0, 128), pl.ds(128, 128)

    def load(src, dst, sem):
        pltpu.make_async_copy(src, dst, sem).start()

    def load13(a, b, e, base, count):
        def step(t, _):
            col = pl.ds(pl.multiple_of(t * 128, 128), 128)
            load(a.at[e, :, col], W13.at[base + t, :, L0], wsem.at[base + t])
            load(b.at[e, :, col], W13.at[base + t, :, L1], wsem.at[base + t])
            return 0
        lax.fori_loop(0, count, step, 0)

    load13(w1_hbm, w3_hbm, 0, 0, nt)
    load13(w1_hbm, w3_hbm, 1, nt, nt)
    sbase = lax.rem(dev, SHARED_DEVS) * 256
    for t in range(2):
        col = pl.ds(pl.multiple_of(sbase + t * 128, 128), 128)
        load(s1_hbm.at[:, col], W13.at[2 * nt + t, :, L0], wsem.at[2 * nt + t])
        load(s3_hbm.at[:, col], W13.at[2 * nt + t, :, L1], wsem.at[2 * nt + t])
    scol = pl.ds(pl.multiple_of(sbase, 256), 256)

    def load2(t, _):
        col = pl.ds(pl.multiple_of(t * 256, 256), 256)
        for e in range(2):
            load(w2_hbm.at[e, :, col], W2.at[t, e], w2sem.at[t])
        load(s2_hbm.at[scol, col], S2.at[t], s2sem.at[t])
        return 0
    lax.fori_loop(0, d // 256, load2, 0)

    def got(ref, sem):
        pltpu.make_async_copy(ref, ref, sem).wait()

    u = _rms(h_ref[...], ln_ref[...])
    U[rows(0, 0, 0), :] = u
    lane = lax.broadcasted_iota(jnp.int32, (bdev, 128), 1)
    oh = jnp.zeros((bdev, 128), F32)
    gm = jnp.zeros((bdev, 128), F32)
    for j in range(idx_ref.shape[1]):
        hit = idx_ref[:, j:j + 1] == lane
        oh = oh + jnp.where(hit, 1.0, 0.0)
        gm = gm + jnp.where(hit, gate_ref[:, j:j + 1], 0.0)
    r_i = lax.broadcasted_iota(jnp.int32, (bdev, bdev), 0)
    c_i = lax.broadcasted_iota(jnp.int32, (bdev, bdev), 1)
    tril = jnp.where(c_i < r_i, 1.0, 0.0)
    rank = jnp.dot(tril.astype(BF16), oh.astype(BF16), preferred_element_type=F32)
    GW[rows(0, 0, 0), :] = jnp.where(rank < cap - 0.5, gm, 0.0)

    SC0 = jax.named_scope
    barrier = pltpu.get_barrier_semaphore()
    for n in (core, xn, yn, zp[1], zp[2], zp[3]):
        pl.semaphore_signal(barrier, inc=1, device_id=n, device_id_type=MESH)
    with SC0("barrier"):
        pl.semaphore_wait(barrier, 6)

    class send:
        def __init__(self, *args):
            self.args = args
            self.make().start()

        def make(self):
            src, dst, ss, rs, to = self.args
            return pltpu.make_async_remote_copy(src_ref=src(), dst_ref=dst(), send_sem=ss(), recv_sem=rs(),
                                                device_id=to, device_id_type=MESH)

        def wait_recv(self):
            self.make().wait_recv()

        def wait_send(self):
            self.make().wait_send()

    sent = []

    ag = {}

    def ag_send(key, i, src_rows, dst_rows, cols, to):
        cp = send(lambda: U.at[src_rows, cols], lambda: U.at[dst_rows, cols], lambda: ag_s.at[i], lambda: ag_r.at[i], to)
        ag[key] = cp
        sent.append(cp)

    gw = {}

    def gw_send(key, i, src_rows, dst_rows, to):
        cp = send(lambda: GW.at[src_rows, :], lambda: GW.at[dst_rows, :], lambda: gw_s.at[i], lambda: gw_r.at[i], to)
        gw[key] = cp
        sent.append(cp)

    def a2(k):
        ag_send(("2x", k), 3 + k * 6, rows(k, 0, 0), rows(k, 0, 1), H0, xn)
        ag_send(("2y", k), 4 + k * 6, rows(k, 0, 0), rows(k, 0, 2), H1, yn)
        gw_send(("2", k), 3 + k * 3, rows(k, 0, 0), rows(k, 0, 1), xn)

    def a3(k):
        ag[("2x", k)].wait_recv()
        ag_send(("3y", k), 5 + k * 6, rows(k, 0, 0, 2), rows(k, 0, 2, 2), H0, yn)
        ag[("2y", k)].wait_recv()
        ag_send(("3x", k), 6 + k * 6, rows(k, 0, 0), rows(k, 0, 1), H1, xn)
        ag_send(("3d", k), 7 + k * 6, rows(k, 0, 2), rows(k, 0, 3), H1, xn)
        gw[("2", k)].wait_recv()
        gw_send(("3", k), 4 + k * 3, rows(k, 0, 0, 2), rows(k, 0, 2, 2), yn)

    def a4(k):
        for n in ("3y", "3x", "3d"):
            ag[(n, k)].wait_recv()
        ag_send(("4", k), 8 + k * 6, rows(k, 0, 0, 4), rows(k, 1, 0, 4), ALL, core)
        gw[("3", k)].wait_recv()
        gw_send(("4", k), 5 + k * 3, rows(k, 0, 0, 4), rows(k, 1, 0, 4), core)

    def a5(k):
        ag[("4", k)].wait_recv()
        gw[("4", k)].wait_recv()

    def zwait(k):
        ag[("z", k)].wait_recv()
        gw[("z", k)].wait_recv()
        a2(k)

    SC = jax.named_scope
    with SC("ag_start"):
        for k in (1, 2, 3):
            ag_send(("z", k), k - 1, rows(0, 0, 0), rows(k, 0, 0), ALL, zp[k])
            gw_send(("z", k), k - 1, rows(0, 0, 0), rows(k, 0, 0), zp[k])
        a2(0)
    with SC("ag_z1"):
        zwait(1)
    with SC("ag_30"):
        a3(0)
    with SC("ag_z2"):
        zwait(2)
    with SC("ag_31"):
        a3(1)
    with SC("ag_z3"):
        zwait(3)
    with SC("ag_41"):
        a4(1)
    with SC("ag_32"):
        a3(2)

    rs = {}

    def rs_send(key, i, src, dst, to):
        cp = send(src, dst, lambda: rs_s.at[i], lambda: rs_r.at[i], to)
        rs[key] = cp
        sent.append(cp)

    COLS = (H0, H1)

    def s1(k, hh):
        cs = COLS[hh]
        rs_send(("1", k, hh), k * 10 + hh, lambda: Pb.at[rows(k, 1, 0, 4), cs], lambda: R1.at[pl.ds(k * 64, 64), cs], core)

    def s2(k, hh):
        cs = COLS[hh]
        rs[("1", k, hh)].wait_recv()
        Pb[rows(k, 0, 0, 4), cs] = Pb[rows(k, 0, 0, 4), cs] + R1[pl.ds(k * 64, 64), cs]
        if hh == 0:
            rs_send(("2y", k), k * 10 + 2, lambda: Pb.at[rows(k, 0, 2, 2), H0], lambda: R2y.at[pl.ds(k * 32, 32), :], yn)
        else:
            rs_send(("2d", k), k * 10 + 3, lambda: Pb.at[rows(k, 0, 3), H1], lambda: R2x.at[pl.ds(k * 32 + 16, 16), :], xn)
            rs_send(("2x", k), k * 10 + 4, lambda: Pb.at[rows(k, 0, 1), H1], lambda: R2x.at[pl.ds(k * 32, 16), :], xn)

    def s3(k, hh):
        if hh == 0:
            rs[("2y", k)].wait_recv()
            Pb[rows(k, 0, 1), H0] = Pb[rows(k, 0, 1), H0] + R2y[pl.ds(k * 32 + 16, 16), :]
            rs_send(("3x", k), k * 10 + 5, lambda: Pb.at[rows(k, 0, 1), H0], lambda: R3x.at[pl.ds(k * 16, 16), :], xn)
            Pb[rows(k, 0, 0), H0] = Pb[rows(k, 0, 0), H0] + R2y[pl.ds(k * 32, 16), :]
        else:
            rs[("2d", k)].wait_recv()
            Pb[rows(k, 0, 2), H1] = Pb[rows(k, 0, 2), H1] + R2x[pl.ds(k * 32 + 16, 16), :]
            rs_send(("3y", k), k * 10 + 6, lambda: Pb.at[rows(k, 0, 2), H1], lambda: R3y.at[pl.ds(k * 16, 16), :], yn)
            rs[("2x", k)].wait_recv()
            Pb[rows(k, 0, 0), H1] = Pb[rows(k, 0, 0), H1] + R2x[pl.ds(k * 32, 16), :]

    def s4(k, hh):
        cs = COLS[hh]
        part = R3x if hh == 0 else R3y
        rs[("3x" if hh == 0 else "3y", k)].wait_recv()
        Pb[rows(k, 0, 0), cs] = Pb[rows(k, 0, 0), cs] + part[pl.ds(k * 16, 16), :]
        if k:
            rs_send(("4", k, hh), k * 10 + 7 + hh, lambda: Pb.at[rows(k, 0, 0), cs], lambda: R4.at[pl.ds(k * 16, 16), cs], zp[k])

    def chunk(ci, k0, n, first, hooks):
        m = n * 8 * bdev
        cr = pl.ds(k0 * 8 * bdev, m)
        mr = pl.ds(0, m)
        lanes = lax.broadcasted_iota(jnp.int32, (m, 128), 1)
        steps = (2 * nt + 2) // UNROLL

        def hook(i):
            if hooks.get(i):
                with SC(f"c{ci}_hook{i}"):
                    for fn, *a in hooks[i]:
                        fn(*a)

        def up(t):
            zz = jnp.dot(U[cr, :], W13[t], preferred_element_type=F32)
            z1, z3 = zz[:, :128], zz[:, 128:]
            g = z1 * jax.nn.sigmoid(z1) * z3
            g = jnp.where((t < 2 * nt) | (dev < SHARED_DEVS), g, 0.0)
            G[mr, pl.ds(pl.multiple_of(t * 128, 128), 128)] = g.astype(BF16)

        def ups(t, _):
            if first:
                for v in range(UNROLL):
                    got(W13.at[t * UNROLL + v], wsem.at[t * UNROLL + v])
            for v in range(UNROLL):
                up(t * UNROLL + v)
            for p in range(steps - 1):
                if hooks.get(p):
                    @pl.when(t == p)
                    def _(p=p):
                        hook(p)
            return 0

        def down(t):
            acc = jnp.dot(G[mr, pl.ds(2 * f, 256)], S2[t], preferred_element_type=F32)
            for e in range(2):
                r = jnp.dot(G[mr, pl.ds(e * f, f)], W2[t, e], preferred_element_type=F32).astype(BF16).astype(F32)
                g = GB[e, mr, :]
                g = jnp.concatenate([g, g], axis=1)
                acc = acc + jnp.where(g > 0, g * r, 0.0)
            Pb[cr, pl.ds(pl.multiple_of(t * 256, 256), 256)] = acc

        def downs(t, _):
            if first:
                for v in range(UNROLL2):
                    got(W2.at[t * UNROLL2 + v], w2sem.at[t * UNROLL2 + v])
                    got(S2.at[t * UNROLL2 + v], s2sem.at[t * UNROLL2 + v])
            for v in range(UNROLL2):
                down(t * UNROLL2 + v)

            if hooks.get(3):
                @pl.when(t == 0)
                def _():
                    hook(3)
            return 0

        with SC(f"c{ci}_gates"):
            for e in range(2):
                gv = jnp.sum(jnp.where(lanes == dev * 2 + e, GW[cr, :], 0.0), axis=1, keepdims=True)
                GB[e, mr, :] = jnp.broadcast_to(gv, (m, 128))
        with SC(f"c{ci}_up"):
            lax.fori_loop(0, steps, ups, 0)
        hook(2)
        with SC(f"c{ci}_down"):
            lax.fori_loop(0, (d // 256) // UNROLL2, downs, 0)
        hook(4)

    for ci, (k0, n) in enumerate(CHUNKS):
        for k in range(k0, k0 + n):
            with SC(f"c{ci}_a5"):
                a5(k)
        chunk(ci, k0, n, ci == 0, HOOKS(ci, a2, zwait, a3, a4, a5, s1, s2, s3, s4))
    ka, kb = CHUNKS[-2][0], CHUNKS[-1][0]
    with SC("t_s2"):
        s2(kb, 0)
        s2(kb, 1)
    with SC("t_s4a"):
        s4(ka, 0)
        s4(ka, 1)
    with SC("t_s3"):
        s3(kb, 0)
        s3(kb, 1)
    with SC("t_s4"):
        s4(kb, 0)
        s4(kb, 1)

    acc = h_ref[...].astype(F32) + Pb[rows(0, 0, 0), :]
    for k in (1, 2, 3):
        with SC(f"t_s5{k}"):
            rs[("4", k, 0)].wait_recv()
            rs[("4", k, 1)].wait_recv()
        acc = acc + R4[pl.ds(k * 16, 16), :]
    y_ref[...] = acc.astype(BF16)
    for cp in sent:
        cp.wait_send()


def solution(mesh):
    def body(x, kv_k, kv_v, lens, idx, gates, ln1, wq, wo, ln2, ws1, ws3, ws2, w1, w3, w2):
        bdev, d = x.shape
        f = w1.shape[2]
        rows = bdev * 32
        h = _attention_block(x, kv_k, kv_v, lens, ln1, wq, wo)
        vm = pl.BlockSpec(memory_space=pltpu.VMEM)
        hbm = pl.BlockSpec(memory_space=pl.ANY)
        mmax = max(n for _, n in CHUNKS) * 8 * bdev
        return pl.pallas_call(
            _moe_kernel,
            out_shape=jax.ShapeDtypeStruct((bdev, d), BF16),
            in_specs=[vm] * 4 + [hbm] * 6,
            out_specs=vm,
            scratch_shapes=[
                pltpu.VMEM((rows, d), BF16),
                pltpu.VMEM((rows, 128), F32),
                pltpu.VMEM((2, mmax, 128), F32),
                pltpu.VMEM((rows, d), F32),
                pltpu.VMEM((rows // 2, d), F32),
                pltpu.VMEM((128, d // 2), F32),
                pltpu.VMEM((128, d // 2), F32),
                pltpu.VMEM((64, d // 2), F32),
                pltpu.VMEM((64, d // 2), F32),
                pltpu.VMEM((64, d), F32),
                pltpu.VMEM((mmax, 2 * f + 256), BF16),
                pltpu.VMEM((2 * f // 128 + 2, d, 256), BF16),
                pltpu.VMEM((d // 256, 2, f, 256), BF16),
                pltpu.VMEM((d // 256, 256, 256), BF16),
                pltpu.SemaphoreType.DMA((2 * f // 128 + 2,)),
                pltpu.SemaphoreType.DMA((d // 256,)),
                pltpu.SemaphoreType.DMA((d // 256,)),
                pltpu.SemaphoreType.DMA((28,)),
                pltpu.SemaphoreType.DMA((28,)),
                pltpu.SemaphoreType.DMA((16,)),
                pltpu.SemaphoreType.DMA((16,)),
                pltpu.SemaphoreType.DMA((40,)),
                pltpu.SemaphoreType.DMA((40,)),
            ],
            compiler_params=pltpu.CompilerParams(
                collective_id=0, has_side_effects=True, vmem_limit_bytes=60 * 1024 * 1024
            ),
        )(h, ln2.reshape(1, d), idx, gates, ws1, ws3, ws2, w1, w3, w2)

    rows = P(GRP)
    rep = P()
    return jax.shard_map(
        body, mesh=mesh,
        in_specs=(rows, rows, rows, rows, rows, rows, rep, rep, rep, rep, rep, rep, rep, rows, rows, rows),
        out_specs=rows, check_vma=False)
```

time: 110 us -> 87.3 us (0.79)
  Pallas kernels: 81.2 us -> 58.2 us
    pallas_call x1, Pallas kernels: 81.2 us -> 58.2 us  [body(): pl.pallas_call(_moe_kernel, out_shape=jax.ShapeDtypeStruct((bdev, d), BF1...]
where the time goes in v2:
time: 87.3 us; the launch traced here: 86.9 us
  Pallas kernels  58.2 us (67%)
  matrix products  23.4 us (27%)
  local copies, waits for them, and re-layouts  3.48 us (4%)
  other arithmetic  1.74 us (2%)
    pallas_call x1, Pallas kernels, body(): pl.pallas_call(_moe_kernel, out_shape=jax.ShapeDtypeStruct((bdev, d), BF1...  58.2 us
    dot_general x1, matrix products, _attention_block(): attn = jnp.dot(o.reshape(b, nh * hd), wo, preferred_element_type=F32)  8.72 us
    dot_general x1, matrix products, _attention_block(): jnp.dot(a, wq, preferred_element_type=F32).astype(BF16)  8.17 us
    sub x1, matrix products, _attention_block(): p = jax.nn.softmax(s, axis=-1).astype(BF16)  3.56 us
    dot_general x1, matrix products, _attention_block(): jnp.einsum('bkgl,blkh->bkgh', p, kv_v, preferred_element_type=F32)  2.92 us
    unnamed x14, local copies, waits for them, and re-layouts  2.88 us

profile of v2, /device:TPU:0, one launch (start us, length us, event | category | flops | bytes accessed | tf_op | source)
XLA Modules:
  0.0 86.9 jit_solution(14355045585308378331)
XLA Ops:
  0.0 0.7 convert_element_type.23
  0.7 1.0 %fusion.19 = f32[16]{0:T(128)S(1)} fusion(bf16[16,2048]{1,0:T(8,128)(2,1)} %param.16), kind=kLoop, calls=%fused_computation.18 | loop fusion | flops 98288 | bytes 65600 | tf_op jit(solution)/shard_map/reduce_sum | solution.py:41
  1.7 0.0 copy-start.4
  1.7 0.0 copy-start
  1.7 8.2 %fusion.17 = bf16[2,8,32,128]{3,1,2,0:T(8,128)(2,1)S(1)} fusion(bf16[2048,4096]{1,0:T(8,128)(2,1)} %param.23, bf16[16,2048]{1,0:T(8,128)(2,1)} %param.16, f32[2048]{0:T(1024)S(1)} %convert_element_type.23, f32[16]{0:T(128)S(1)} %add_rsqrt_fusion), kind=kOutput, calls=%fused_computation.13 | convolution fusion | flops 268632064 | bytes 16982080 | tf_op jit(solution)/shard_map/dot_general | solution.py:50
  9.9 0.0 copy-done.4
  9.9 0.1 iota_compare_fusion
  10.0 3.6 %fusion.27 = (f32[16,4,8]{2,1,0:T(4,128)S(1)}, f32[16,4,8,256]{3,2,1,0:T(8,128)S(1)}) fusion(bf16[16,4,8,128]{3,2,1,0:T(8,128)(2,1)S(1)} %bitcast.13, bf16[16,256,4,128]{3,2,1,0:T(4,128)(2,1)} %param.17, pred[16,256]{1,0:T(8,128)(4,1)S(1)} %iota_compare_fusion), kind=kOutput, calls=%fused_computation.27 | convolution fusion | flops 34078976 | bytes 4855808 | tf_op jit(solution)/shard_map/sub | solution.py:53
  13.5 2.9 %fusion.14 = bf16[16,4,8,128]{3,2,1,0:T(8,128)(2,1)S(1)} fusion(bf16[16,256,4,128]{3,2,1,0:T(4,128)(2,1)} %param.18, f32[16,4,8,256]{3,2,1,0:T(8,128)S(1)} %get-tuple-element.6, f32[16,4,8]{2,1,0:T(4,128)S(1)} %get-tuple-element.5), kind=kOutput, calls=%fused_computation.12 | convolution fusion | flops 33882112 | bytes 4851712 | tf_op jit(solution)/shard_map/bkgl,blkh->bkgh/dot_general | solution.py:54
  16.4 0.0 copy-done
  16.4 0.0 copy-start.2
  16.5 0.0 copy-start.3
  16.5 0.0 copy-start.1
  16.5 8.7 %fusion.5.h_ref = bf16[16,2048]{1,0:T(8,128)(2,1)} fusion(bf16[4096,2048]{1,0:T(8,128)(2,1)} %param.24, bf16[16,2048]{1,0:T(8,128)(2,1)S(1)} %copy-done, bf16[2,8,32,128]{3,2,1,0:T(8,128)(2,1)S(1)} %bitcast.12), kind=kOutput, calls=%fused_computation.7 | convolution fusion | flops 268533760 | bytes 17039360 | tf_op jit(solution)/shard_map/dot_general | solution.py:55
  25.2 0.0 copy-done.2
  25.2 0.7 copy.19.idx_ref
  25.9 0.0 copy-done.3
  25.9 0.7 copy.20.gate_ref
  26.6 0.0 copy-done.1
  26.6 0.6 reshape.43.ln_ref
  27.2 58.2 %shard_map.154 = bf16[16,2048]{1,0:T(8,128)(2,1)} custom-call(bf16[16,2048]{1,0:T(8,128)(2,1)} %fusion.5.h_ref, bf16[1,2048]{1,0:T(2,128)(2,1)} %reshape.43.ln_ref, s32[16,4]{1,0:T(8,128)} %copy.19.idx_ref, f32[16,4]{1,0:T(8,128)} %copy.20.gate_ref, bf16[2048,5632]{1,0:T(8,128)(2,1)} %s1_hbm.1, bf16[2048,5632]{1,0:T(8,128)(2,1)} %s3_hbm.1, ...), custom_call_target="tpu_custom_call" | custom-call | tf_op jit(solution)/shard_map/pallas_call | solution.py:371
  85.4 1.5 %copy.40 = bf16[16,2048]{1,0:T(8,128)(2,1)} copy(bf16[16,2048]{1,0:T(8,128)(2,1)} %shard_map.154) | data formatting | bytes 131072
  (2 shorter events, 0.0 us)
Async XLA Ops:
  1.7 8.2 %copy-start.4 = (s32[16]{0:T(128)S(1)}, s32[16]{0:T(128)}, u32[]{:S(2)}) copy-start(s32[16]{0:T(128)} %param.19) | copy-start | bytes 196
  1.7 14.8 %copy-start = (bf16[16,2048]{1,0:T(8,128)(2,1)S(1)}, bf16[16,2048]{1,0:T(8,128)(2,1)}, u32[]{:S(2)}) copy-start(bf16[16,2048]{1,0:T(8,128)(2,1)} %param.16) | copy-start | bytes 196612
  16.4 8.8 %copy-start.2 = (s32[16,4]{0,1:T(4,128)S(1)}, s32[16,4]{0,1:T(4,128)}, u32[]{:S(2)}) copy-start(s32[16,4]{0,1:T(4,128)} %param.20) | copy-start | bytes 772
  16.5 9.4 %copy-start.3 = (f32[16,4]{0,1:T(4,128)S(1)}, f32[16,4]{0,1:T(4,128)}, u32[]{:S(2)}) copy-start(f32[16,4]{0,1:T(4,128)} %param.21) | copy-start | bytes 772
  16.5 10.1 %copy-start.1 = (bf16[2048]{0:T(1024)(128)(2,1)S(1)}, bf16[2048]{0:T(1024)(128)(2,1)}, u32[]{:S(2)}) copy-start(bf16[2048]{0:T(1024)(128)(2,1)} %param.25) | copy-start | bytes 12292

commit v3 on v0

v3 whole, which is shorter than its diff:
```python
import functools

import jax
import jax.numpy as jnp
from jax import lax
from jax.experimental import pallas as pl
from jax.experimental.pallas import tpu as pltpu
from jax.sharding import PartitionSpec as P

EPS = 1e-6
GRP = ("ey", "ex")
MESH = pl.DeviceIdType.MESH
BF16, F32 = jnp.bfloat16, jnp.float32

LANES, TILE = 128, 256


def _loop(n, step):
    def body(t, carry):
        step(t)
        return carry
    lax.fori_loop(0, n, body, 0)


def _at(t, width):
    return pl.ds(pl.multiple_of(t * width, width), width)


SHARED_DEVS = 22
CHUNKS = ((1, 1), (2, 1), (3, 1), (0, 1))
UNROLL, UNROLL2 = 8, 4


def HOOKS(ci, a2, zwait, a3, a4, a5, s1, s2, s3, s4):
    order = [k for k, _ in CHUNKS]
    k = order[ci]
    ev = {i: [] for i in range(5)}
    if ci == 0:
        ev[1] += [(a3, 3), (a4, 2)]
        ev[2] += [(a4, 0)]
        ev[4] += [(a4, 3)]
    if ci >= 2:
        ev[1] += [(s4, order[ci - 2], 0), (s4, order[ci - 2], 1)]
    if ci >= 1:
        ev[0] += [(s2, order[ci - 1], 0), (s2, order[ci - 1], 1)]
    ev[3] += [(s1, k, 0)]
    ev[4] += [(s1, k, 1)]
    if ci >= 1:
        ev[4] += [(s3, order[ci - 1], 0), (s3, order[ci - 1], 1)]
    return ev


def _norm(v, ln_ref):
    r = lax.rsqrt(jnp.mean(v * v, axis=-1, keepdims=True) + EPS)
    n = v.shape[1] // 128
    return jnp.concatenate(
        [(v[:, i * 128:(i + 1) * 128] * r * ln_ref[i:i + 1, :].astype(F32)).astype(BF16) for i in range(n)], axis=1)


def _attend(lens_ref, x_ref, ln1_ref, ln2_ref, k_hbm, v_hbm, wq_hbm, wo_hbm, h_ref, u_ref, between,
            WQ, WO, K, V, QS, OS, A, ACC, POS, qsem, osem, ksem, vsem):
    b, d = x_ref.shape
    hd = LANES
    nh = wq_hbm.shape[1] // hd
    rows = K.shape[1]
    kvh = rows // 256
    grp = nh // kvh
    nq, no, nk = qsem.shape[0], osem.shape[0], ksem.shape[0]
    cq, co, ck = d // nq, (nh * hd) // no, b // nk

    def cpq(i):
        return pltpu.make_async_copy(wq_hbm.at[_at(i, cq), :], WQ.at[_at(i, cq), :], qsem.at[i])

    def cpo(i):
        return pltpu.make_async_copy(wo_hbm.at[_at(i, co), :], WO.at[_at(i, co), :], osem.at[i])

    def cpk(i):
        return pltpu.make_async_copy(k_hbm.at[pl.ds(i * ck, ck)], K.at[pl.ds(i * ck, ck)], ksem.at[i])

    def cpv(i):
        return pltpu.make_async_copy(v_hbm.at[pl.ds(i * ck, ck)], V.at[pl.ds(i * ck, ck)], vsem.at[i])

    _loop(nq, lambda i: cpq(i).start())
    xf = x_ref[...].astype(F32)
    A[...] = _norm(xf, ln1_ref)
    ACC[...] = jnp.zeros(ACC.shape, F32)
    row = lax.broadcasted_iota(jnp.int32, (rows, LANES), 0)
    lane = lax.broadcasted_iota(jnp.int32, (rows, LANES), 1)
    own = lax.rem(row, kvh) == lax.div(lax.rem(lane, nh), grp)
    POS[...] = jnp.where(own, lax.div(row, kvh), 1 << 20)
    between[0]()

    def queries(i):
        cpq(i).wait()

        @pl.when(i >= nq - nk)
        def _():
            cpk(i - (nq - nk)).start()
            cpv(i - (nq - nk)).start()
        ACC[...] = ACC[...] + jnp.dot(A[:, _at(i, cq)], WQ[_at(i, cq), :], preferred_element_type=F32)
    _loop(nq, queries)
    _loop(no, lambda i: cpo(i).start())
    for i in range(nh):
        QS[i * b:(i + 1) * b, :] = ACC[:, i * hd:(i + 1) * hd].astype(BF16).astype(F32)
    between[1]()

    lane1 = lax.div(lax.broadcasted_iota(jnp.int32, (1, LANES), 1), nh)
    slot = lax.div(lax.broadcasted_iota(jnp.int32, (LANES, LANES), 1), nh)
    scale = hd ** -0.5 * 1.4426950408889634

    def group(g):
        cpk(g).wait()
        cpv(g).wait()
        first = g * ck
        q = jnp.concatenate([QS[pl.ds(first + i, nh, stride=b), :] for i in range(ck)], axis=0)
        qt = jnp.transpose(q)
        qq = jnp.concatenate([jnp.where(slot == i, qt, 0.0).astype(BF16) for i in range(ck)], axis=0)
        kc = jnp.concatenate([K[first + i] for i in range(ck)], axis=1)
        s = jnp.dot(kc, qq, preferred_element_type=F32)
        n = jnp.zeros(lane1.shape, jnp.int32)
        for i in range(ck):
            n = jnp.where(lane1 == i, lens_ref[first + i], n)
        s = jnp.where(POS[...] < n, s, -jnp.inf)
        p = jnp.exp2((s - jnp.max(s, axis=0, keepdims=True)) * scale)
        p = (p * (1.0 / jnp.sum(p, axis=0, keepdims=True))).astype(BF16)
        pt = jnp.transpose(p)
        for i in range(ck):
            o = jnp.dot(pt[i * nh:(i + 1) * nh, :], V[first + i], preferred_element_type=F32)
            OS[pl.ds(first + i, nh, stride=b), :] = o.astype(BF16).astype(F32)
    _loop(nk, group)
    between[2]()

    ACC[:, 0:d] = jnp.zeros((b, d), F32)

    def outs(i):
        cpo(i).wait()
        n = co // hd
        o = jnp.concatenate([OS[pl.ds(pl.multiple_of((i * n + j) * b, b), b), :].astype(BF16) for j in range(n)], axis=1)
        ACC[:, 0:d] = ACC[:, 0:d] + jnp.dot(o, WO[_at(i, co), :], preferred_element_type=F32)
    _loop(no, outs)
    h = (xf + ACC[:, 0:d]).astype(BF16)
    h_ref[...] = h
    u_ref[...] = _norm(h.astype(F32), ln2_ref)


def _gates(idx_ref, gate_ref, gw_ref, IDX, GT):
    top, b = idx_ref.shape
    cap = b - b // 8
    IDX[...] = jnp.zeros(IDX.shape, jnp.int32)
    GT[...] = jnp.zeros(GT.shape, F32)
    IDX[0:top, 0:b] = idx_ref[...]
    GT[0:top, 0:b] = gate_ref[...]
    expert = lax.broadcasted_iota(jnp.int32, (LANES, LANES), 0)
    oh = jnp.zeros((LANES, LANES), F32)
    gm = jnp.zeros((LANES, LANES), F32)
    for j in range(top):
        hit = IDX[j:j + 1, :] == expert
        oh = oh + jnp.where(hit, 1.0, 0.0)
        gm = gm + jnp.where(hit, GT[j:j + 1, :], 0.0)
    before = jnp.where(expert < lax.broadcasted_iota(jnp.int32, (LANES, LANES), 1), 1.0, 0.0)
    rank = jnp.dot(oh.astype(BF16), before.astype(BF16), preferred_element_type=F32)
    gw_ref[...] = jnp.transpose(jnp.where(rank < cap - 0.5, gm, 0.0))[0:b, :]


def _layer_kernel(lens_ref, x_ref, ln1_ref, ln2_ref, idx_ref, gate_ref, k_hbm, v_hbm, wq_hbm, wo_hbm,
                  s1_hbm, s3_hbm, s2_hbm, w1_hbm, w3_hbm, w2_hbm, y_ref, h_ref, IDX, GT,
                  U, GW, R1, R2x, R2y, R3x, R3y, R4,
                  ag_s, ag_r, gw_s, gw_r, rs_s, rs_r):
    z = lax.axis_index("ey")
    ex = lax.axis_index("ex")
    c = lax.rem(ex, 2)
    xx = lax.rem(lax.div(ex, 2), 2)
    yy = lax.div(ex, 4)
    dev = z * 8 + ex
    bdev, d = x_ref.shape
    f = w1_hbm.shape[2]
    half = d // 2
    H0, H1 = pl.ds(0, half), pl.ds(half, half)
    ALL = pl.ds(0, d)
    core = (z, ex + 1 - 2 * c)
    xn = (z, ex + 2 - 4 * xx)
    yn = (z, ex + 4 - 8 * yy)
    zp = {1: (z + 1 - 2 * lax.rem(z, 2), ex), 2: (z + 2 - 4 * lax.div(z, 2), ex), 3: (3 - z, ex)}

    def rows(k, dc, dq, n=1):
        return pl.ds(((k * 2 + dc) * 4 + dq) * bdev, n * bdev)

    _gates(idx_ref, gate_ref, GW.at[rows(0, 0, 0), :], IDX, GT)

    SC0 = jax.named_scope
    barrier = pltpu.get_barrier_semaphore()
    for n in (core, xn, yn, zp[1], zp[2], zp[3]):
        pl.semaphore_signal(barrier, inc=1, device_id=n, device_id_type=MESH)
    with SC0("barrier"):
        pl.semaphore_wait(barrier, 6)

    class send:
        def __init__(self, *args):
            self.args = args
            self.make().start()

        def make(self):
            src, dst, ss, rs, to = self.args
            return pltpu.make_async_remote_copy(src_ref=src(), dst_ref=dst(), send_sem=ss(), recv_sem=rs(),
                                                device_id=to, device_id_type=MESH)

        def wait_recv(self):
            self.make().wait_recv()

        def wait_send(self):
            self.make().wait_send()

    sent = []

    def flush():
        for cp in sent:
            cp.wait_send()
        sent.clear()

    ag = {}

    def ag_send(key, i, src_rows, dst_rows, cols, to):
        cp = send(lambda: U.at[src_rows, cols], lambda: U.at[dst_rows, cols], lambda: ag_s.at[i], lambda: ag_r.at[i], to)
        ag[key] = cp
        sent.append(cp)

    gw = {}

    def gw_send(key, i, src_rows, dst_rows, to):
        cp = send(lambda: GW.at[src_rows, :], lambda: GW.at[dst_rows, :], lambda: gw_s.at[i], lambda: gw_r.at[i], to)
        gw[key] = cp
        sent.append(cp)

    def a2(k, hh):
        cs = (H0, H1)[hh]
        near, far = (xn, yn) if hh == 0 else (yn, xn)
        nd, fd = (1, 2) if hh == 0 else (2, 1)
        ag_send(("2", k, hh), 6 + k * 8 + hh, rows(k, 0, 0), rows(k, 0, nd), cs, near)
        ag_send(("3", k, hh), 8 + k * 8 + hh, rows(k, 0, 0), rows(k, 0, fd), cs, far)

    def g1():
        for k in (1, 2, 3):
            gw_send(("z", k), k - 1, rows(0, 0, 0), rows(k, 0, 0), zp[k])

    def g2():
        for k in range(4):
            if k:
                gw[("z", k)].wait_recv()
            gw_send(("2", k), 3 + k * 3, rows(k, 0, 0), rows(k, 0, 1), xn)

    def g3():
        for k in range(4):
            gw[("2", k)].wait_recv()
            gw_send(("3", k), 4 + k * 3, rows(k, 0, 0, 2), rows(k, 0, 2, 2), yn)

    def g4():
        for k in range(4):
            gw[("3", k)].wait_recv()
            gw_send(("4", k), 5 + k * 3, rows(k, 0, 0, 4), rows(k, 1, 0, 4), core)

    def a3(k):
        ag[("2", k, 0)].wait_recv()
        ag_send(("4", k, 0), 10 + k * 8, rows(k, 0, 1), rows(k, 0, 3), H0, yn)
        ag[("2", k, 1)].wait_recv()
        ag_send(("4", k, 1), 11 + k * 8, rows(k, 0, 2), rows(k, 0, 3), H1, xn)

    def a4(k):
        for hh in range(2):
            ag[("3", k, hh)].wait_recv()
        ag_send(("5", k), 12 + k * 8, rows(k, 0, 0, 3), rows(k, 1, 0, 3), ALL, core)
        for hh in range(2):
            ag[("4", k, hh)].wait_recv()
        ag_send(("6", k), 13 + k * 8, rows(k, 0, 3), rows(k, 1, 3), ALL, core)

    def a5(k):
        ag[("5", k)].wait_recv()
        ag[("6", k)].wait_recv()

    def zwait(k):
        for hh in range(2):
            ag[("z", k, hh)].wait_recv()
            a2(k, hh)

    nh, l4 = wq_hbm.shape[1] // LANES, k_hbm.shape[1]
    pl.run_scoped(
        functools.partial(_attend, lens_ref, x_ref, ln1_ref, ln2_ref, k_hbm, v_hbm, wq_hbm, wo_hbm, h_ref,
                          U.at[rows(0, 0, 0), :], (g1, g2, g3)),
        pltpu.VMEM(wq_hbm.shape, BF16),
        pltpu.VMEM(wo_hbm.shape, BF16),
        pltpu.VMEM(k_hbm.shape, BF16),
        pltpu.VMEM(k_hbm.shape, BF16),
        pltpu.VMEM((nh * bdev, LANES), F32),
        pltpu.VMEM((nh * bdev, LANES), F32),
        pltpu.VMEM((bdev, d), BF16),
        pltpu.VMEM((bdev, nh * LANES), F32),
        pltpu.VMEM((l4, LANES), jnp.int32),
        pltpu.SemaphoreType.DMA((8,)),
        pltpu.SemaphoreType.DMA((8,)),
        pltpu.SemaphoreType.DMA((4,)),
        pltpu.SemaphoreType.DMA((4,)),
    )

    def experts(GB, Pb, G, W13, W2, S2, wsem, w2sem, s2sem):
        with SC0("ag_start"):
            for k in (1, 2, 3):
                for hh in range(2):
                    ag_send(("z", k, hh), (k - 1) * 2 + hh, rows(0, 0, 0), rows(k, 0, 0), (H0, H1)[hh], zp[k])
            a2(0, 0)
            a2(0, 1)
        nt = f // 128
        L0, L1 = pl.ds(0, LANES), pl.ds(LANES, LANES)

        def load(src, dst, sem):
            pltpu.make_async_copy(src, dst, sem).start()

        def load13(a, b, e, base, count):
            def step(t):
                col = _at(t, LANES)
                load(a.at[e, :, col], W13.at[base + t, :, L0], wsem.at[base + t])
                load(b.at[e, :, col], W13.at[base + t, :, L1], wsem.at[base + t])
            _loop(count, step)

        load13(w1_hbm, w3_hbm, 0, 0, nt)
        load13(w1_hbm, w3_hbm, 1, nt, nt)
        sbase = lax.rem(dev, SHARED_DEVS) * 2
        for t in range(2):
            col = _at(sbase + t, LANES)
            load(s1_hbm.at[:, col], W13.at[2 * nt + t, :, L0], wsem.at[2 * nt + t])
            load(s3_hbm.at[:, col], W13.at[2 * nt + t, :, L1], wsem.at[2 * nt + t])
        scol = _at(sbase // 2, TILE)

        def load2(t):
            col = _at(t, TILE)
            for e in range(2):
                load(w2_hbm.at[e, :, col], W2.at[t, e], w2sem.at[t])
            load(s2_hbm.at[scol, col], S2.at[t], s2sem.at[t])
        _loop(d // TILE, load2)

        def got(ref, sem):
            pltpu.make_async_copy(ref, ref, sem).wait()

        g4()
        with SC0("ag_z1"):
            zwait(1)
        with SC0("ag_30"):
            a3(0)
        with SC0("ag_z2"):
            zwait(2)
        with SC0("ag_31"):
            a3(1)
        with SC0("ag_z3"):
            zwait(3)
        with SC0("ag_41"):
            a4(1)
        with SC0("ag_32"):
            a3(2)

        rs = {}

        def rs_send(key, i, src, dst, to):
            cp = send(src, dst, lambda: rs_s.at[i], lambda: rs_r.at[i], to)
            rs[key] = cp
            sent.append(cp)

        COLS = (H0, H1)

        def s1(k, hh):
            cs = COLS[hh]
            rs_send(("1", k, hh), k * 10 + hh, lambda: Pb.at[rows(k, 1, 0, 4), cs], lambda: R1.at[pl.ds(k * 64, 64), cs], core)

        def s2(k, hh):
            cs = COLS[hh]
            rs[("1", k, hh)].wait_recv()
            Pb[rows(k, 0, 0, 4), cs] = Pb[rows(k, 0, 0, 4), cs] + R1[pl.ds(k * 64, 64), cs]
            if hh == 0:
                rs_send(("2y", k), k * 10 + 2, lambda: Pb.at[rows(k, 0, 2, 2), H0], lambda: R2y.at[pl.ds(k * 32, 32), :], yn)
            else:
                rs_send(("2d", k), k * 10 + 3, lambda: Pb.at[rows(k, 0, 3), H1], lambda: R2x.at[pl.ds(k * 32 + 16, 16), :], xn)
                rs_send(("2x", k), k * 10 + 4, lambda: Pb.at[rows(k, 0, 1), H1], lambda: R2x.at[pl.ds(k * 32, 16), :], xn)

        def s3(k, hh):
            if hh == 0:
                rs[("2y", k)].wait_recv()
                Pb[rows(k, 0, 1), H0] = Pb[rows(k, 0, 1), H0] + R2y[pl.ds(k * 32 + 16, 16), :]
                rs_send(("3x", k), k * 10 + 5, lambda: Pb.at[rows(k, 0, 1), H0], lambda: R3x.at[pl.ds(k * 16, 16), :], xn)
                Pb[rows(k, 0, 0), H0] = Pb[rows(k, 0, 0), H0] + R2y[pl.ds(k * 32, 16), :]
            else:
                rs[("2d", k)].wait_recv()
                Pb[rows(k, 0, 2), H1] = Pb[rows(k, 0, 2), H1] + R2x[pl.ds(k * 32 + 16, 16), :]
                rs_send(("3y", k), k * 10 + 6, lambda: Pb.at[rows(k, 0, 2), H1], lambda: R3y.at[pl.ds(k * 16, 16), :], yn)
                rs[("2x", k)].wait_recv()
                Pb[rows(k, 0, 0), H1] = Pb[rows(k, 0, 0), H1] + R2x[pl.ds(k * 32, 16), :]

        def s4(k, hh):
            cs = COLS[hh]
            part = R3x if hh == 0 else R3y
            rs[("3x" if hh == 0 else "3y", k)].wait_recv()
            Pb[rows(k, 0, 0), cs] = Pb[rows(k, 0, 0), cs] + part[pl.ds(k * 16, 16), :]
            if k:
                rs_send(("4", k, hh), k * 10 + 7 + hh, lambda: Pb.at[rows(k, 0, 0), cs], lambda: R4.at[pl.ds(k * 16, 16), cs], zp[k])

        SC = jax.named_scope
        def chunk(ci, k0, n, first, hooks):
            m = n * 8 * bdev
            cr = pl.ds(k0 * 8 * bdev, m)
            mr = pl.ds(0, m)
            lanes = lax.broadcasted_iota(jnp.int32, (m, LANES), 1)
            steps = (2 * nt + 2) // UNROLL

            def hook(i):
                if hooks.get(i):
                    with SC(f"c{ci}_hook{i}"):
                        for fn, *a in hooks[i]:
                            fn(*a)

            def up(t):
                zz = jnp.dot(U[cr, :], W13[t], preferred_element_type=F32)
                z1, z3 = zz[:, :128], zz[:, 128:]
                g = z1 * jax.nn.sigmoid(z1) * z3
                g = jnp.where((t < 2 * nt) | (dev < SHARED_DEVS), g, 0.0)
                G[mr, _at(t, LANES)] = g.astype(BF16)

            def ups(t):
                if first:
                    for v in range(UNROLL):
                        got(W13.at[t * UNROLL + v], wsem.at[t * UNROLL + v])
                for v in range(UNROLL):
                    up(t * UNROLL + v)
                for p in range(steps - 1):
                    if hooks.get(p):
                        @pl.when(t == p)
                        def _(p=p):
                            hook(p)

            def down(t):
                acc = jnp.dot(G[mr, pl.ds(2 * f, 256)], S2[t], preferred_element_type=F32)
                for e in range(2):
                    r = jnp.dot(G[mr, pl.ds(e * f, f)], W2[t, e], preferred_element_type=F32).astype(BF16).astype(F32)
                    g = GB[e, mr, :]
                    g = jnp.concatenate([g, g], axis=1)
                    acc = acc + jnp.where(g > 0, g * r, 0.0)
                Pb[cr, _at(t, TILE)] = acc

            def downs(t):
                if first:
                    for v in range(UNROLL2):
                        got(W2.at[t * UNROLL2 + v], w2sem.at[t * UNROLL2 + v])
                        got(S2.at[t * UNROLL2 + v], s2sem.at[t * UNROLL2 + v])
                for v in range(UNROLL2):
                    down(t * UNROLL2 + v)

                if hooks.get(3):
                    @pl.when(t == 0)
                    def _():
                        hook(3)

            with SC(f"c{ci}_gates"):
                for e in range(2):
                    gv = jnp.sum(jnp.where(lanes == dev * 2 + e, GW[cr, :], 0.0), axis=1, keepdims=True)
                    GB[e, mr, :] = jnp.broadcast_to(gv, (m, LANES))
            with SC(f"c{ci}_up"):
                _loop(steps, ups)
            if ci == len(CHUNKS) - 1:
                flush()
            hook(2)
            with SC(f"c{ci}_down"):
                _loop(d // TILE // UNROLL2, downs)
            hook(4)

        for ci, (k0, n) in enumerate(CHUNKS):
            for k in range(k0, k0 + n):
                with SC(f"c{ci}_a5"):
                    a5(k)
                    gw[("4", k)].wait_recv()
            chunk(ci, k0, n, ci == 0, HOOKS(ci, a2, zwait, a3, a4, a5, s1, s2, s3, s4))
        ka, kb = CHUNKS[-2][0], CHUNKS[-1][0]
        with SC("t_s2"):
            s2(kb, 0)
            s2(kb, 1)
        with SC("t_s4a"):
            s4(ka, 0)
            s4(ka, 1)
        with SC("t_s3"):
            s3(kb, 0)
            s3(kb, 1)
        with SC("t_s4"):
            s4(kb, 0)
            s4(kb, 1)

        acc = h_ref[...].astype(F32) + Pb[rows(0, 0, 0), :]
        for k in (1, 2, 3):
            with SC(f"t_s5{k}"):
                rs[("4", k, 0)].wait_recv()
                rs[("4", k, 1)].wait_recv()
            acc = acc + R4[pl.ds(k * 16, 16), :]
        y_ref[...] = acc.astype(BF16)
        flush()

    mmax = max(n for _, n in CHUNKS) * 8 * bdev
    f = w1_hbm.shape[2]
    pl.run_scoped(
        experts,
        pltpu.VMEM((2, mmax, LANES), F32),
        pltpu.VMEM((bdev * 32, d), F32),
        pltpu.VMEM((mmax, 2 * f + TILE), BF16),
        pltpu.VMEM((2 * f // LANES + 2, d, TILE), BF16),
        pltpu.VMEM((d // TILE, 2, f, TILE), BF16),
        pltpu.VMEM((d // TILE, TILE, TILE), BF16),
        pltpu.SemaphoreType.DMA((2 * f // LANES + 2,)),
        pltpu.SemaphoreType.DMA((d // TILE,)),
        pltpu.SemaphoreType.DMA((d // TILE,)),
    )


def solution(mesh):
    def body(x, kv_k, kv_v, lens, idx, gates, ln1, wq, wo, ln2, ws1, ws3, ws2, w1, w3, w2):
        bdev, d = x.shape
        _, l, kvh, hd = kv_k.shape
        rows = bdev * 32
        vm = pl.BlockSpec(memory_space=pltpu.VMEM)
        hbm = pl.BlockSpec(memory_space=pl.ANY)
        kv = (bdev, l * kvh, hd)
        sem = pltpu.SemaphoreType.DMA
        return pl.pallas_call(
            _layer_kernel,
            out_shape=jax.ShapeDtypeStruct((bdev, d), BF16),
            in_specs=[pl.BlockSpec(memory_space=pltpu.SMEM)] + [vm] * 5 + [hbm] * 10,
            out_specs=vm,
            scratch_shapes=[
                pltpu.VMEM((bdev, d), BF16),
                pltpu.VMEM((8, LANES), jnp.int32),
                pltpu.VMEM((8, LANES), F32),
                pltpu.VMEM((rows, d), BF16),
                pltpu.VMEM((rows, LANES), F32),
                pltpu.VMEM((rows // 2, d), F32),
                pltpu.VMEM((rows // 4, d // 2), F32),
                pltpu.VMEM((rows // 4, d // 2), F32),
                pltpu.VMEM((rows // 8, d // 2), F32),
                pltpu.VMEM((rows // 8, d // 2), F32),
                pltpu.VMEM((rows // 8, d), F32),
                sem((38,)), sem((38,)), sem((16,)), sem((16,)), sem((40,)), sem((40,)),
            ],
            compiler_params=pltpu.CompilerParams(
                collective_id=0, has_side_effects=True, vmem_limit_bytes=62 * 1024 * 1024
            ),
        )(lens, x, ln1.reshape(d // LANES, LANES), ln2.reshape(d // LANES, LANES), idx.T, gates.T,
          kv_k.reshape(kv), kv_v.reshape(kv), wq, wo, ws1, ws3, ws2, w1, w3, w2)

    rows = P(GRP)
    rep = P()
    return jax.shard_map(
        body, mesh=mesh,
        in_specs=(rows, rows, rows, rows, rows, rows, rep, rep, rep, rep, rep, rep, rep, rows, rows, rows),
        out_specs=rows, check_vma=False)
```

time: 344 us -> 75.7 us (0.22)
  waiting for transfers between devices: 179 us -> 0 us
  matrix products: 75.9 us -> 0 us
  Pallas kernels: 0 us -> 73.3 us
  local copies, waits for them, and re-layouts: 57.6 us -> 1.47 us
  starting transfers between devices: 17.4 us -> 0 us
  other arithmetic: 12.9 us -> 0 us
    all_to_all x3 -> x0, waiting for transfers between devices: 179 us -> none  [the longest x1 93.4 us: body(): recv_rows = lax.all_to_all(send_rows, GRP, 0, 0, tiled=True)]
    pallas_call x0 -> x1, Pallas kernels: none -> 73.3 us  [body(): pl.pallas_call(_layer_kernel, out_shape=jax.ShapeDtypeStruct((bdev, d), B...]
    dot_general x8 -> x0, matrix products: 72.4 us -> none  [the longest x1 17.9 us: _swiglu(): return jnp.dot(g, w2, preferred_element_type=jnp.float32)]
    gather x6 -> x0, local copies, waits for them, and re-layouts: 31.6 us -> none  [the longest x2 17.1 us: body(): jnp.take(out, recv_meta, axis=0, mode='fill', fill_value=0)]
    all_to_all x3 -> x0, starting transfers between devices: 17.4 us -> none  [the longest x1 7.36 us: body(): recv_meta = lax.all_to_all(send_meta, GRP, 0, 0, tiled=True).reshape(-1)]
    reshape x4 -> x0, local copies, waits for them, and re-layouts: 11.9 us -> none  [the longest x1 5.84 us: body(): recv_rows.reshape(-1, d)]
    scatter x3 -> x0, local copies, waits for them, and re-layouts: 11.7 us -> none  [the longest x1 10.1 us: body(): jnp.zeros((edev * qrows, d), jnp.bfloat16).at[recv_meta]]
    select_n x6 -> x0, other arithmetic: 9.08 us -> none  [the longest x2 4.53 us: body(): jnp.take(out, recv_meta, axis=0, mode='fill', fill_value=0)]
  transfers between devices with their start and end apart: 3 -> 0, of which waited for: 2 -> 0; matrix products, arithmetic and copies ran while one was open for 15% -> 0% of each run, Pallas kernels for 0% -> 0%
where the time goes in v3:
time: 75.7 us; the launch traced here: 74.8 us
  Pallas kernels  73.3 us (97%)
  local copies, waits for them, and re-layouts  1.47 us (2%)
    pallas_call x1, Pallas kernels, body(): pl.pallas_call(_layer_kernel, out_shape=jax.ShapeDtypeStruct((bdev, d), B...  73.3 us

profile of v3, /device:TPU:0, one launch (start us, length us, event | category | flops | bytes accessed | tf_op | source)
XLA Modules:
  0.0 74.8 jit_solution(12047846409610214402)
XLA Ops:
  0.0 73.3 %shard_map.154 = bf16[16,2048]{1,0:T(8,128)(2,1)} custom-call(s32[16]{0:T(128)} %lens_ref.1, bf16[16,2048]{1,0:T(8,128)(2,1)} %x_ref.1, bf16[16,128]{1,0:T(8,128)(2,1)} %bitcast.8, bf16[16,128]{1,0:T(8,128)(2,1)} %bitcast.9, s32[4,16]{1,0:T(4,128)} %bitcast.10, f32[4,16]{1,0:T(4,128)} %bitcast.11, bf16[16,1024,128]{2,1,0:T(8,128)(2,1)} %bitcast.6, ...), custom_call_target="tpu_custom_call" | custom-call | tf_op jit(solution)/shard_map/pallas_call | solution.py:524
  73.3 1.5 %copy.18 = bf16[16,2048]{1,0:T(8,128)(2,1)} copy(bf16[16,2048]{1,0:T(8,128)(2,1)} %shard_map.154) | data formatting | bytes 131072

commit v4 on v3

--- a/solution.py
+++ b/solution.py
@@ -28,7 +28,7 @@
 
 SHARED_DEVS = 22
 CHUNKS = ((1, 1), (2, 1), (3, 1), (0, 1))
-UNROLL, UNROLL2 = 8, 4
+UNROLL, UNROLL2, PAIR = 12, 8, 1
 
 
 def HOOKS(ci, a2, zwait, a3, a4, a5, s1, s2, s3, s4):
@@ -36,11 +36,11 @@
     k = order[ci]
     ev = {i: [] for i in range(5)}
     if ci == 0:
-        ev[1] += [(a3, 3), (a4, 2)]
+        ev[0] += [(a3, 3), (a4, 2)]
         ev[2] += [(a4, 0)]
         ev[4] += [(a4, 3)]
     if ci >= 2:
-        ev[1] += [(s4, order[ci - 2], 0), (s4, order[ci - 2], 1)]
+        ev[2] += [(s4, order[ci - 2], 0), (s4, order[ci - 2], 1)]
     if ci >= 1:
         ev[0] += [(s2, order[ci - 1], 0), (s2, order[ci - 1], 1)]
     ev[3] += [(s1, k, 0)]
@@ -109,8 +109,6 @@
     scale = hd ** -0.5 * 1.4426950408889634
 
     def group(g):
-        cpk(g).wait()
-        cpv(g).wait()
         first = g * ck
         q = jnp.concatenate([QS[pl.ds(first + i, nh, stride=b), :] for i in range(ck)], axis=0)
         qt = jnp.transpose(q)
@@ -127,17 +125,29 @@
         for i in range(ck):
             o = jnp.dot(pt[i * nh:(i + 1) * nh, :], V[first + i], preferred_element_type=F32)
             OS[pl.ds(first + i, nh, stride=b), :] = o.astype(BF16).astype(F32)
-    _loop(nk, group)
+    def groups(t):
+        for g in range(PAIR):
+            cpk(t * PAIR + g).wait()
+            cpv(t * PAIR + g).wait()
+        for g in range(PAIR):
+            group(t * PAIR + g)
+    _loop(nk // PAIR, groups)
     between[2]()
 
     ACC[:, 0:d] = jnp.zeros((b, d), F32)
 
-    def outs(i):
+    for i in range(no):
         cpo(i).wait()
+
+    def outs(t):
         n = co // hd
-        o = jnp.concatenate([OS[pl.ds(pl.multiple_of((i * n + j) * b, b), b), :].astype(BF16) for j in range(n)], axis=1)
-        ACC[:, 0:d] = ACC[:, 0:d] + jnp.dot(o, WO[_at(i, co), :], preferred_element_type=F32)
-    _loop(no, outs)
+        part = ACC[:, 0:d]
+        for v in range(no // 2):
+            i = t * (no // 2) + v
+            o = jnp.concatenate([OS[_at(i * n + j, b), :].astype(BF16) for j in range(n)], axis=1)
+            part = part + jnp.dot(o, WO[_at(i, co), :], preferred_element_type=F32)
+        ACC[:, 0:d] = part
+    _loop(2, outs)
     h = (xf + ACC[:, 0:d]).astype(BF16)
     h_ref[...] = h
     u_ref[...] = _norm(h.astype(F32), ln2_ref)
@@ -185,14 +195,13 @@
     def rows(k, dc, dq, n=1):
         return pl.ds(((k * 2 + dc) * 4 + dq) * bdev, n * bdev)
 
-    _gates(idx_ref, gate_ref, GW.at[rows(0, 0, 0), :], IDX, GT)
-
     SC0 = jax.named_scope
     barrier = pltpu.get_barrier_semaphore()
-    for n in (core, xn, yn, zp[1], zp[2], zp[3]):
-        pl.semaphore_signal(barrier, inc=1, device_id=n, device_id_type=MESH)
-    with SC0("barrier"):
-        pl.semaphore_wait(barrier, 6)
+
+    def g0():
+        for n in (core, xn, yn, zp[1], zp[2], zp[3]):
+            pl.semaphore_signal(barrier, inc=1, device_id=n, device_id_type=MESH)
+        _gates(idx_ref, gate_ref, GW.at[rows(0, 0, 0), :], IDX, GT)
 
     class send:
         def __init__(self, *args):
@@ -239,6 +248,8 @@
         ag_send(("3", k, hh), 8 + k * 8 + hh, rows(k, 0, 0), rows(k, 0, fd), cs, far)
 
     def g1():
+        with SC0("barrier"):
+            pl.semaphore_wait(barrier, 6)
         for k in (1, 2, 3):
             gw_send(("z", k), k - 1, rows(0, 0, 0), rows(k, 0, 0), zp[k])
 
@@ -284,7 +295,7 @@
     nh, l4 = wq_hbm.shape[1] // LANES, k_hbm.shape[1]
     pl.run_scoped(
         functools.partial(_attend, lens_ref, x_ref, ln1_ref, ln2_ref, k_hbm, v_hbm, wq_hbm, wo_hbm, h_ref,
-                          U.at[rows(0, 0, 0), :], (g1, g2, g3)),
+                          U.at[rows(0, 0, 0), :], (g0, g1, g2)),
         pltpu.VMEM(wq_hbm.shape, BF16),
         pltpu.VMEM(wo_hbm.shape, BF16),
         pltpu.VMEM(k_hbm.shape, BF16),
@@ -307,6 +318,7 @@
                     ag_send(("z", k, hh), (k - 1) * 2 + hh, rows(0, 0, 0), rows(k, 0, 0), (H0, H1)[hh], zp[k])
             a2(0, 0)
             a2(0, 1)
+            g3()
         nt = f // 128
         L0, L1 = pl.ds(0, LANES), pl.ds(LANES, LANES)
 
@@ -339,7 +351,6 @@
         def got(ref, sem):
             pltpu.make_async_copy(ref, ref, sem).wait()
 
-        g4()
         with SC0("ag_z1"):
             zwait(1)
         with SC0("ag_30"):
@@ -354,6 +365,7 @@
             a4(1)
         with SC0("ag_32"):
             a3(2)
+        g4()
 
         rs = {}
 
@@ -406,6 +418,8 @@
             mr = pl.ds(0, m)
             lanes = lax.broadcasted_iota(jnp.int32, (m, LANES), 1)
             steps = (2 * nt + 2) // UNROLL
+            last = ci == len(CHUNKS) - 1
+            un2 = UNROLL2 // 2 if last else UNROLL2
 
             def hook(i):
                 if hooks.get(i):
@@ -443,13 +457,13 @@
 
             def downs(t):
                 if first:
-                    for v in range(UNROLL2):
-                        got(W2.at[t * UNROLL2 + v], w2sem.at[t * UNROLL2 + v])
-                        got(S2.at[t * UNROLL2 + v], s2sem.at[t * UNROLL2 + v])
-                for v in range(UNROLL2):
-                    down(t * UNROLL2 + v)
-
-                if hooks.get(3):
+                    for v in range(un2):
+                        got(W2.at[t * un2 + v], w2sem.at[t * un2 + v])
+                        got(S2.at[t * un2 + v], s2sem.at[t * un2 + v])
+                for v in range(un2):
+                    down(t * un2 + v)
+
+                if hooks.get(3) and last:
                     @pl.when(t == 0)
                     def _():
                         hook(3)
@@ -460,11 +474,13 @@
                     GB[e, mr, :] = jnp.broadcast_to(gv, (m, LANES))
             with SC(f"c{ci}_up"):
                 _loop(steps, ups)
-            if ci == len(CHUNKS) - 1:
+            if last:
                 flush()
             hook(2)
             with SC(f"c{ci}_down"):
-                _loop(d // TILE // UNROLL2, downs)
+                _loop(d // TILE // un2, downs)
+            if not last:
+                hook(3)
             hook(4)
 
         for ci, (k0, n) in enumerate(CHUNKS):

time: 75.7 us -> 71.5 us (0.945)
  Pallas kernels: 73.3 us -> 69.8 us
    pallas_call x1, Pallas kernels: 73.3 us -> 69.8 us  [body(): pl.pallas_call(_layer_kernel, out_shape=jax.ShapeDtypeStruct((bdev, d), B...]
where the time goes in v4:
time: 71.5 us; the launch traced here: 71.3 us
  Pallas kernels  69.8 us (98%)
  local copies, waits for them, and re-layouts  1.47 us (2%)
    pallas_call x1, Pallas kernels, body(): pl.pallas_call(_layer_kernel, out_shape=jax.ShapeDtypeStruct((bdev, d), B...  69.8 us
    unnamed x1, local copies, waits for them, and re-layouts  1.47 us

profile of v4, /device:TPU:0, one launch (start us, length us, event | category | flops | bytes accessed | tf_op | source)
XLA Modules:
  0.0 71.3 jit_solution(3802779067360080956)
XLA Ops:
  0.0 69.8 %shard_map.154 = bf16[16,2048]{1,0:T(8,128)(2,1)} custom-call(s32[16]{0:T(128)} %lens_ref.1, bf16[16,2048]{1,0:T(8,128)(2,1)} %x_ref.1, bf16[16,128]{1,0:T(8,128)(2,1)} %bitcast.8, bf16[16,128]{1,0:T(8,128)(2,1)} %bitcast.9, s32[4,16]{1,0:T(4,128)} %bitcast.10, f32[4,16]{1,0:T(4,128)} %bitcast.11, bf16[16,1024,128]{2,1,0:T(8,128)(2,1)} %bitcast.6, ...), custom_call_target="tpu_custom_call" | custom-call | tf_op jit(solution)/shard_map/pallas_call | solution.py:540
  69.8 1.5 %copy.18 = bf16[16,2048]{1,0:T(8,128)(2,1)} copy(bf16[16,2048]{1,0:T(8,128)(2,1)} %shard_map.154) | data formatting | bytes 131072

commit v5 on v4

--- a/solution.py
+++ b/solution.py
@@ -136,18 +136,12 @@
 
     ACC[:, 0:d] = jnp.zeros((b, d), F32)
 
-    for i in range(no):
+    def outs(i):
         cpo(i).wait()
-
-    def outs(t):
         n = co // hd
-        part = ACC[:, 0:d]
-        for v in range(no // 2):
-            i = t * (no // 2) + v
-            o = jnp.concatenate([OS[_at(i * n + j, b), :].astype(BF16) for j in range(n)], axis=1)
-            part = part + jnp.dot(o, WO[_at(i, co), :], preferred_element_type=F32)
-        ACC[:, 0:d] = part
-    _loop(2, outs)
+        o = jnp.concatenate([OS[pl.ds(pl.multiple_of((i * n + j) * b, b), b), :].astype(BF16) for j in range(n)], axis=1)
+        ACC[:, 0:d] = ACC[:, 0:d] + jnp.dot(o, WO[_at(i, co), :], preferred_element_type=F32)
+    _loop(no, outs)
     h = (xf + ACC[:, 0:d]).astype(BF16)
     h_ref[...] = h
     u_ref[...] = _norm(h.astype(F32), ln2_ref)

time: 71.5 us -> 70.6 us (0.987)
  Pallas kernels: 69.8 us -> 68.9 us
    pallas_call x1, Pallas kernels: 69.8 us -> 68.9 us  [body(): pl.pallas_call(_layer_kernel, out_shape=jax.ShapeDtypeStruct((bdev, d), B...]
where the time goes in v5:
time: 70.6 us; the launch traced here: 70.4 us
  Pallas kernels  68.9 us (98%)
  local copies, waits for them, and re-layouts  1.47 us (2%)
    pallas_call x1, Pallas kernels, body(): pl.pallas_call(_layer_kernel, out_shape=jax.ShapeDtypeStruct((bdev, d), B...  68.9 us
    unnamed x1, local copies, waits for them, and re-layouts  1.47 us

profile of v5, /device:TPU:0, one launch (start us, length us, event | category | flops | bytes accessed | tf_op | source)
XLA Modules:
  0.0 70.4 jit_solution(17718710546736970769)
XLA Ops:
  0.0 68.9 %shard_map.154 = bf16[16,2048]{1,0:T(8,128)(2,1)} custom-call(s32[16]{0:T(128)} %lens_ref.1, bf16[16,2048]{1,0:T(8,128)(2,1)} %x_ref.1, bf16[16,128]{1,0:T(8,128)(2,1)} %bitcast.8, bf16[16,128]{1,0:T(8,128)(2,1)} %bitcast.9, s32[4,16]{1,0:T(4,128)} %bitcast.10, f32[4,16]{1,0:T(4,128)} %bitcast.11, bf16[16,1024,128]{2,1,0:T(8,128)(2,1)} %bitcast.6, ...), custom_call_target="tpu_custom_call" | custom-call | tf_op jit(solution)/shard_map/pallas_call | solution.py:534
  69.0 1.5 %copy.18 = bf16[16,2048]{1,0:T(8,128)(2,1)} copy(bf16[16,2048]{1,0:T(8,128)(2,1)} %shard_map.154) | data formatting | bytes 131072
